TPU v7x, 32 devices: a whole 2x2x4 slice. The times are simulated.
32 devices in a mesh: samp: 4 (over x, core), snp: 8 (over z, y).
Axes of the slice: x: 2, y: 2, z: 4, core: 2. Of those that a mesh axis runs over, the one named last changes fastest.
Arguments:
- genotypes: float32 [4096, 8192], P('samp', 'snp'), may hold values from -1 to 2, as said below
Outputs:
- band_r: float32 [8192, 4096], P('snp', 'samp')
Inputs may be any that keep to these rules, and one draw needn't show every extreme that they name: `genotypes`: -1 marks a missing dosage; every other value lies between 0 and 2. Every eighth sample (samples 0, 8, 16, ...) has no missing dosage, and over those samples each SNP's dosages run through 0, 1, 2 cyclically from a SNP's own starting value.
All inputs are finite; a program needn't handle non-finite values.
Results may differ from a plain program's by a relative error of at most 0.006.
Values may be sent and summed in bfloat16 or wider, within the bound.
No kernel may reach another device: no remote copies, remote signals or barrier semaphores. Data moves between devices by JAX's collectives and lax.ppermute only.
A program may use at most 64 MiB of HBM per device.

v0:
```python
import jax
import jax.numpy as jnp
from jax import lax
from jax.sharding import PartitionSpec as P

TILE = 512
BAND = 4096


EPS = 1e-05


def passed_along(x, axis, by):
    count = lax.axis_size(axis)
    pairs = [(i, i + by) for i in range(count) if 0 <= i + by < count]
    return lax.ppermute(x, axis, pairs)


def on_device(genotypes):
    present = (genotypes >= 0).astype(jnp.float32)
    dosage = genotypes * present
    counted, summed, squared = lax.psum(
        (jnp.sum(present, axis=0), jnp.sum(dosage, axis=0), jnp.sum(dosage * dosage, axis=0)),
        "samp",
    )
    average = summed / counted
    spread = squared / counted - average * average
    scaled = (present * (dosage - average) * lax.rsqrt(spread + EPS)).astype(jnp.bfloat16)
    col_norms = counted * spread / (spread + EPS)
    snp_dev = genotypes.shape[1]
    tiles_dev = snp_dev // TILE
    panels = (BAND - TILE + 2 * snp_dev - 1) // snp_dev - 1
    span_cols = (panels + 1) * snp_dev
    pieces = [scaled]
    norm_pieces = [col_norms]
    current = scaled
    current_norm = col_norms
    for distance in range(1, panels + 1):
        current = passed_along(current, "snp", -1)
        pieces.append(current)
        current_norm = passed_along(current_norm, "snp", -1)
        norm_pieces.append(current_norm)
    extended = jnp.concatenate(pieces, axis=1)
    device_pos = lax.axis_index("snp")
    far_norms = jnp.concatenate(norm_pieces)
    columns = device_pos * snp_dev + jnp.arange(span_cols, dtype=jnp.int32)
    inside = columns < lax.axis_size("snp") * snp_dev
    far_norms = jnp.where(inside, far_norms, 1.0)
    quarter = BAND // lax.axis_size("samp")
    partial_value = []
    for tile_pos in range(tiles_dev):
        row_block = scaled[:, tile_pos * TILE : (tile_pos + 1) * TILE]
        col_block = extended[:, tile_pos * TILE : tile_pos * TILE + BAND]
        partial_value.append(
            lax.dot_general(
                row_block, col_block, (((0,), (0,)), ((), ())), preferred_element_type=jnp.float32
            )
        )
    summed_tiles = jnp.concatenate(partial_value, axis=0)
    shares = lax.psum_scatter(summed_tiles, "samp", scatter_dimension=1, tiled=True)
    samp_pos = lax.axis_index("samp")
    results = []
    for tile_pos in range(tiles_dev):
        col_norm = lax.dynamic_slice_in_dim(
            far_norms, tile_pos * TILE + samp_pos * quarter, quarter, 0
        )
        row_norm = col_norms[tile_pos * TILE : (tile_pos + 1) * TILE]
        block_share = shares[tile_pos * TILE : (tile_pos + 1) * TILE]
        results.append(block_share / jnp.sqrt(row_norm[:, None] * col_norm[None, :]))
    return jnp.concatenate(results, axis=0)


def solution(mesh):
    in_specs = (P("samp", "snp"),)
    out_specs = P("snp", "samp")
    return jax.shard_map(
        on_device, mesh=mesh, in_specs=in_specs, out_specs=out_specs, check_vma=False
    )
```

profile of v0, /device:TPU:0, one launch (start us, length us, event | category | flops | bytes accessed | tf_op | source)
XLA Modules:
  0.0 372.0 jit_solution(1408418810053538005)
XLA Ops:
  6.5 3.2 multiply_reduce_fusion
  9.7 12.6 %all-reduce = (f32[1024]{0:T(1024)S(1)}, f32[1024]{0:T(1024)S(1)}, f32[1024]{0:T(1024)S(1)}) all-reduce(f32[1024]{0:T(1024)S(1)} %get-tuple-element.6, f32[1024]{0:T(1024)S(1)} %get-tuple-element.7, f32[1024]{0:T(1024)S(1)} %get-tuple-element.5), channel_id=1, replica_groups=mesh['samp'=4,'snp'=8] {'samp'}, use_global_device_ids=true, to_apply=%region_1.0 | all-reduce | flops 3072 | bytes 24576 | tf_op jit(solution)/shard_map/psum | solution.py:22
  22.4 3.1 constant_dynamic-update-slice_fusion.4
  25.5 1.3 collective-permute-start
  26.8 46.4 %collective-permute-done = bf16[1024,1024]{1,0:T(8,128)(2,1)S(1)} collective-permute-done((bf16[1024,1024]{1,0:T(8,128)(2,1)S(1)}, bf16[1024,1024]{1,0:T(8,128)(2,1)S(1)}, u32[]{:S(2)}, u32[]{:S(2)}) %collective-permute-start) | collective-permute-done | bytes 2097184 | tf_op jit(solution)/shard_map/ppermute | solution.py:16
  73.2 1.3 collective-permute-start.1
  74.5 46.4 %collective-permute-done.1 = bf16[1024,1024]{1,0:T(8,128)(2,1)S(1)} collective-permute-done((bf16[1024,1024]{1,0:T(8,128)(2,1)S(1)}, bf16[1024,1024]{1,0:T(8,128)(2,1)S(1)}, u32[]{:S(2)}, u32[]{:S(2)}) %collective-permute-start.1) | collective-permute-done | bytes 2097184 | tf_op jit(solution)/shard_map/ppermute | solution.py:16
  120.9 1.3 collective-permute-start.2
  122.2 45.8 %collective-permute-done.2 = bf16[1024,1024]{1,0:T(8,128)(2,1)} collective-permute-done((bf16[1024,1024]{1,0:T(8,128)(2,1)S(1)}, bf16[1024,1024]{1,0:T(8,128)(2,1)}, u32[]{:S(2)}, u32[]{:S(2)}) %collective-permute-start.2) | collective-permute-done | bytes 2097184 | tf_op jit(solution)/shard_map/ppermute | solution.py:16
  167.9 1.5 collective-permute-start.3
  169.8 1.8 constant_dynamic-update-slice_fusion.1
  171.5 9.2 %fusion.2 = f32[512,4096]{1,0:T(8,128)} fusion(bf16[1024,1024]{1,0:T(8,128)(2,1)} %collective-permute-done.2, bf16[1024,1024]{1,0:T(8,128)(2,1)} %copy-done, bf16[1024,1024]{1,0:T(8,128)(2,1)S(1)} %collective-permute-done, bf16[1024,1024]{1,0:T(8,128)(2,1)S(1)} %get-tuple-element.15), kind=kOutput, calls=%fused_computation.3 | convolution fusion | flops 4328521728 | bytes 17825792 | tf_op jit(solution)/shard_map/dot_general | solution.py:55
  180.7 33.6 %collective-permute-done.3 = bf16[1024,1024]{1,0:T(8,128)(2,1)} collective-permute-done((bf16[1024,1024]{1,0:T(8,128)(2,1)}, bf16[1024,1024]{1,0:T(8,128)(2,1)}, u32[]{:S(2)}, u32[]{:S(2)}) %collective-permute-start.3) | collective-permute-done | bytes 2097184 | tf_op jit(solution)/shard_map/ppermute | solution.py:16
  214.3 1.8 constant_dynamic-update-slice_fusion
  216.1 4.6 %fusion = f32[512,4096]{1,0:T(8,128)S(1)} fusion(bf16[1024,5120]{1,0:T(8,128)(2,1)S(1)} %constant_dynamic-update-slice_fusion, bf16[1024,1024]{1,0:T(8,128)(2,1)S(1)} %get-tuple-element.15), kind=kOutput, calls=%fused_computation.1 | convolution fusion | flops 4294967296 | bytes 17825792 | tf_op jit(solution)/shard_map/dot_general | solution.py:55
  220.7 10.1 %pad_maximum_fusion = f32[1024,4096]{1,0:T(8,128)} fusion(f32[512,4096]{1,0:T(8,128)S(1)} %fusion, f32[512,4096]{1,0:T(8,128)} %fusion.2), kind=kLoop, calls=%fused_computation | loop fusion | flops 4194304 | bytes 33554432 | tf_op jit(solution)/shard_map/concatenate | solution.py:59
  230.9 1.3 collective-permute-start.4
  232.2 4.8 %collective-permute-done.4 = f32[1024]{0:T(1024)S(1)} collective-permute-done((f32[1024]{0:T(1024)S(1)}, f32[1024]{0:T(1024)S(1)}, u32[]{:S(2)}, u32[]{:S(2)}) %collective-permute-start.4) | collective-permute-done | bytes 4128 | tf_op jit(solution)/shard_map/ppermute | solution.py:16
  238.3 5.1 %collective-permute-done.5 = f32[1024]{0:T(1024)S(1)} collective-permute-done((f32[1024]{0:T(1024)S(1)}, f32[1024]{0:T(1024)S(1)}, u32[]{:S(2)}, u32[]{:S(2)}) %collective-permute-start.5) | collective-permute-done | bytes 4128 | tf_op jit(solution)/shard_map/ppermute | solution.py:16
  243.4 1.3 collective-permute-start.6
  244.7 5.1 %collective-permute-done.6 = f32[1024]{0:T(1024)S(1)} collective-permute-done((f32[1024]{0:T(1024)S(1)}, f32[1024]{0:T(1024)S(1)}, u32[]{:S(2)}, u32[]{:S(2)}) %collective-permute-start.6) | collective-permute-done | bytes 4128 | tf_op jit(solution)/shard_map/ppermute | solution.py:16
  251.1 5.1 %collective-permute-done.7 = f32[1024]{0:T(1024)S(1)} collective-permute-done((f32[1024]{0:T(1024)S(1)}, f32[1024]{0:T(1024)S(1)}, u32[]{:S(2)}, u32[]{:S(2)}) %collective-permute-start.7) | collective-permute-done | bytes 4128 | tf_op jit(solution)/shard_map/ppermute | solution.py:16
  256.3 104.1 %reduce-scatter.2.cloned.1.call-done = f32[1024,1024]{1,0:T(8,128)} async-done(((f32[1024,4096]{1,0:T(8,128)}), f32[1024,1024]{1,0:T(8,128)}) %reduce-scatter.2.cloned.1.call-update) | async-done | bytes 4194320 | tf_op jit(solution)/shard_map/reduce_scatter | solution.py:60
  360.3 4.8 %slice_multiply_fusion.1 = (f32[1024,1024]{1,0:T(8,128)}, f32[1024,1024]{1,0:T(8,128)}) fusion(f32[1024,1024]{1,0:T(8,128)} %reduce-scatter.2.cloned.1.call-done, f32[1024]{0:T(1024)S(1)} %get-tuple-element.18, f32[512]{0:T(512)S(1)} %get-tuple-element.20, f32[1024]{0:T(1024)S(1)} %get-tuple-element.19, ...), kind=kLoop, output_to_operand_aliasing={{0}: (5, {}), {1}: (5, {})}, calls=%fused_computation.16 | loop fusion | flops 2097152 | bytes 8400896 | tf_op jit(solution)/shard_map/div | solution.py:69
  (18 shorter events, 3.1 us)
Async XLA Ops:
  6.5 353.8 %reduce-scatter.2.cloned.1.call-start = ((), (), s32[]{:S(2)}) async-start(), calls=%async_computation.1 | async-start | bytes 20971520 | tf_op jit(solution)/shard_map/reduce_scatter | solution.py:60
  25.5 47.7 %collective-permute-start = (bf16[1024,1024]{1,0:T(8,128)(2,1)S(1)}, bf16[1024,1024]{1,0:T(8,128)(2,1)S(1)}, u32[]{:S(2)}, u32[]{:S(2)}) collective-permute-start(bf16[1024,1024]{1,0:T(8,128)(2,1)S(1)} %get-tuple-element.15), channel_id=1, source_target_pairs={{1,0},{2,1},{3,2},{4,3},{5,4},{6,5},{7,6},{9,8},{10,9},{11,10},{12... | collective-permute-start | bytes 6291464 | tf_op jit(solution)/shard_map/ppermute | solution.py:16
  73.2 47.7 %collective-permute-start.1 = (bf16[1024,1024]{1,0:T(8,128)(2,1)S(1)}, bf16[1024,1024]{1,0:T(8,128)(2,1)S(1)}, u32[]{:S(2)}, u32[]{:S(2)}) collective-permute-start(bf16[1024,1024]{1,0:T(8,128)(2,1)S(1)} %collective-permute-done), channel_id=1, source_target_pairs={{1,0},{2,1},{3,2},{4,3},{5,4},{6,5},{7,6},{9,8},{10,9},{11,10},{12... | collective-permute-start | bytes 6291464 | tf_op jit(solution)/shard_map/ppermute | solution.py:16
  120.9 48.9 %copy-start = (bf16[1024,1024]{1,0:T(8,128)(2,1)}, bf16[1024,1024]{1,0:T(8,128)(2,1)S(1)}, u32[]{:S(2)}) copy-start(bf16[1024,1024]{1,0:T(8,128)(2,1)S(1)} %collective-permute-done.1) | copy-start | bytes 6291460
  120.9 47.1 %collective-permute-start.2 = (bf16[1024,1024]{1,0:T(8,128)(2,1)S(1)}, bf16[1024,1024]{1,0:T(8,128)(2,1)}, u32[]{:S(2)}, u32[]{:S(2)}) collective-permute-start(bf16[1024,1024]{1,0:T(8,128)(2,1)S(1)} %collective-permute-done.1), channel_id=1, source_target_pairs={{1,0},{2,1},{3,2},{4,3},{5,4},{6,5},{7,6},{9,8},{10,9},{11,10},{12... | collective-permute-start | bytes 6291464 | tf_op jit(solution)/shard_map/ppermute | solution.py:16
  167.9 46.4 %collective-permute-start.3 = (bf16[1024,1024]{1,0:T(8,128)(2,1)}, bf16[1024,1024]{1,0:T(8,128)(2,1)}, u32[]{:S(2)}, u32[]{:S(2)}) collective-permute-start(bf16[1024,1024]{1,0:T(8,128)(2,1)} %collective-permute-done.2), channel_id=1, source_target_pairs={{1,0},{2,1},{3,2},{4,3},{5,4},{6,5},{7,6},{9,8},{10,9},{11,10},{12... | collective-permute-start | bytes 6291464 | tf_op jit(solution)/shard_map/ppermute | solution.py:16
  230.9 6.1 %collective-permute-start.4 = (f32[1024]{0:T(1024)S(1)}, f32[1024]{0:T(1024)S(1)}, u32[]{:S(2)}, u32[]{:S(2)}) collective-permute-start(f32[1024]{0:T(1024)S(1)} %get-tuple-element.12), channel_id=1, source_target_pairs={{1,0},{2,1},{3,2},{4,3},{5,4},{6,5},{7,6},{9,8},{10,9},{11,10},{12... | collective-permute-start | bytes 12296 | tf_op jit(solution)/shard_map/ppermute | solution.py:16
  237.0 6.4 %collective-permute-start.5 = (f32[1024]{0:T(1024)S(1)}, f32[1024]{0:T(1024)S(1)}, u32[]{:S(2)}, u32[]{:S(2)}) collective-permute-start(f32[1024]{0:T(1024)S(1)} %collective-permute-done.4), channel_id=1, source_target_pairs={{1,0},{2,1},{3,2},{4,3},{5,4},{6,5},{7,6},{9,8},{10,9},{11,10},{12... | collective-permute-start | bytes 12296 | tf_op jit(solution)/shard_map/ppermute | solution.py:16
  243.4 6.4 %collective-permute-start.6 = (f32[1024]{0:T(1024)S(1)}, f32[1024]{0:T(1024)S(1)}, u32[]{:S(2)}, u32[]{:S(2)}) collective-permute-start(f32[1024]{0:T(1024)S(1)} %collective-permute-done.5), channel_id=1, source_target_pairs={{1,0},{2,1},{3,2},{4,3},{5,4},{6,5},{7,6},{9,8},{10,9},{11,10},{12... | collective-permute-start | bytes 12296 | tf_op jit(solution)/shard_map/ppermute | solution.py:16
  249.8 6.4 %collective-permute-start.7 = (f32[1024]{0:T(1024)S(1)}, f32[1024]{0:T(1024)S(1)}, u32[]{:S(2)}, u32[]{:S(2)}) collective-permute-start(f32[1024]{0:T(1024)S(1)} %collective-permute-done.6), channel_id=1, source_target_pairs={{1,0},{2,1},{3,2},{4,3},{5,4},{6,5},{7,6},{9,8},{10,9},{11,10},{12... | collective-permute-start | bytes 12296 | tf_op jit(solution)/shard_map/ppermute | solution.py:16
Sparse Core Ops, SparseCore 0:
  231.0 129.2 reduce-scatter.1
where the time goes:
time: 372 us
  waiting for transfers between devices  296 us (80%)
  other arithmetic  21.2 us (6%)
  matrix products  13.8 us (4%)
  between operations  13.6 us (4%)
  blocking collectives  12.6 us (3%)
  starting transfers between devices  10.4 us (3%)
  local copies, waits for them, and re-layouts  3.97 us (1%)
    ppermute x8, waiting for transfers between devices, passed_along(): return lax.ppermute(x, axis, pairs)  192 us
    reduce_scatter x1, waiting for transfers between devices, on_device(): lax.psum_scatter(summed_tiles, 'samp', scatter_dimension=1, tiled=True)  104 us
    dot_general x2, matrix products, on_device(): lax.dot_general(row_block, col_block, (((0,), (0,)), ((), ())), preferred...  13.8 us
    psum x1, blocking collectives, on_device(): lax.psum((jnp.sum(present, axis=0), jnp.sum(dosage, axis=0), jnp.sum(dosa...  12.6 us
    ppermute x8, starting transfers between devices, passed_along(): return lax.ppermute(x, axis, pairs)  10.4 us
    concatenate x1, other arithmetic, on_device(): summed_tiles = jnp.concatenate(partial_value, axis=0)  10.1 us
  transfers between devices with their start and end apart: 9, of which 9 were waited for; matrix products, arithmetic and copies ran while one was open for 3% of the time, Pallas kernels for 0%

commit v1 on v0

v1 whole, which is shorter than its diff:
```python
import jax
import jax.numpy as jnp
from jax import lax
from jax.sharding import PartitionSpec as P


TILE = 512
BAND = 4096
WIDTH = TILE // 2


def dot_t(rows, cols):
    return lax.dot_general(rows, cols, (((0,), (0,)), ((), ())), preferred_element_type=jnp.float32)


def make_on_device(samp_size, snp_size):
    axes = ("samp", "snp")

    def perm(x, move):
        pairs = []
        for samp in range(samp_size):
            for p in range(snp_size):
                target = move(samp // 2, samp % 2, p)
                if target is None:
                    continue
                tx, tc, tp = target
                if 0 <= tp < snp_size:
                    pairs.append((samp * snp_size + p, (tx * 2 + tc) * snp_size + tp))
        return lax.ppermute(x, axes, pairs)

    def core_swap(x):
        return perm(x, lambda xx, c, p: (xx, 1 - c, p))

    def x_swap(x):
        return perm(x, lambda xx, c, p: (1 - xx, c, p))

    def to_x0(x):
        return perm(x, lambda xx, c, p: (0, c, p) if xx == 1 else None)

    def to_x1(x):
        return perm(x, lambda xx, c, p: (1, c, p) if xx == 0 else None)

    def relay(c, p, crossed):
        return (c, p + 1) if p % 2 == 0 else (1 - c if crossed else c, p - 1)

    def on_device(genotypes):
        _, snps = genotypes.shape
        assert samp_size == 4 and snp_size % 2 == 0
        assert snps == 2 * TILE and BAND == 4 * snps
        bf16, f32 = jnp.bfloat16, jnp.float32
        samp = lax.axis_index("samp")
        xx, core = samp // 2, samp % 2
        x_first, first_core = xx == 0, core == 0
        even = (lax.axis_index("snp") % 2) == 0

        last = [None]

        def after(x):
            return x if last[0] is None else lax.optimization_barrier((x, last[0]))[0]

        def step(make, *args):
            args = (after(args[0]), *args[1:])
            last[0] = make(*args)
            last[0] = lax.optimization_barrier(last[0])
            return last[0]

        present = (genotypes >= 0).astype(f32)
        dosage = genotypes * present
        stats = jnp.stack([jnp.sum(present, axis=0), jnp.sum(dosage, axis=0), jnp.sum(dosage * dosage, axis=0)])
        stats = stats + core_swap(stats)
        stats = stats + x_swap(stats)
        average = stats[1] / stats[0]
        factor = lax.rsqrt(stats[0] * (stats[2] / stats[0] - average * average))
        scale = lax.optimization_barrier(jnp.stack([average, factor]))

        def columns(x, start):
            return lax.dynamic_slice_in_dim(x, start, WIDTH, 1)

        def standardized(by, g):
            return jnp.where(g >= 0, (g - by[0]) * by[1], 0.0).astype(bf16)

        def staged(x):
            return jnp.maximum(x, jnp.finfo(bf16).min)

        def send_same(j):
            return perm(keep[j], lambda xx, c, p: (xx, c, p - 2))

        def send_cross(j):
            return perm(give[j], lambda xx, c, p: (xx, 1 - c, p - 2))

        def relay_same(j):
            payload = step(lambda e: jnp.where(e, above[j][0], keep[j]), even)
            return perm(payload, lambda xx, c, p: (xx, *relay(c, p, False)))

        def relay_cross(j):
            payload = step(lambda e: jnp.where(e, above[j][1], give[j]), even)
            return perm(payload, lambda xx, c, p: (xx, *relay(c, p, True)))

        def pair(rows, cols):
            return step(lambda r: dot_t(r, cols[0]) + dot_t(rows[1], cols[1]), rows[0])

        keep_start, give_start = core * TILE, (1 - core) * TILE
        keep = [step(lambda by: standardized(columns(by, keep_start), columns(genotypes, keep_start)), scale)]
        above = [[send_same(0)]]
        mine = step(standardized, scale, genotypes)
        up = perm(mine, lambda xx, c, p: (xx, c, p + 2))
        theirs = core_swap(mine)
        give = [step(columns, mine, give_start)]
        above[0].append(send_cross(0))
        nexts = [[relay_same(0)]]
        keep.append(step(columns, mine, keep_start + WIDTH))
        above.append([send_same(1)])
        give.append(step(columns, mine, give_start + WIDTH))
        above[1].append(send_cross(1))
        across = [core_swap(give[j]) for j in (0, 1)]
        nexts[0].append(relay_cross(0))
        rows = (mine, step(staged, theirs))
        d0 = [pair(rows, (keep[j], across[j])) for j in (0, 1)]
        x_d0 = to_x0(jnp.concatenate(d0, axis=0).astype(bf16))
        d2 = [pair(rows, above[0])]
        x_d2 = [to_x1(d2[0].astype(bf16))]
        nexts.append([relay_same(1)])
        d1 = [pair(rows, nexts[0])]
        x_d1 = [to_x0(d1[0].astype(bf16))]
        nexts[1].append(relay_cross(1))
        other_up = core_swap(up)
        d2.append(pair(rows, above[1]))
        x_d2.append(to_x1(d2[1].astype(bf16)))
        below = (step(staged, up), step(staged, other_up))
        z_near, z_far = [], []

        def send_d3(j):
            part = pair(below, nexts[j]).astype(bf16)
            z_near.append(perm(part, lambda xx, c, p: (1, c, p - 2) if xx == 1 else None))
            z_far.append(perm(part, lambda xx, c, p: (1, c, p - 2) if xx == 0 else None))

        send_d3(0)
        below_low = (below[0][:, TILE:], below[1][:, TILE:])
        d4 = jnp.concatenate([pair(below_low, a) for a in above], axis=0).astype(bf16)
        q_near = perm(d4, lambda xx, c, p: (1, 1, p - 2) if (xx, c) == (1, 0) else None)
        q_far = perm(d4, lambda xx, c, p: (1, 1, p - 2) if (xx, c) == (0, 0) else None)
        low = jnp.concatenate([d[TILE:] for d in d2], axis=0).astype(bf16)
        x_low = perm(low, lambda xx, c, p: (0, c, p) if (xx, c) == (1, 0) else None)
        send_d3(1)
        d1.append(pair(rows, nexts[1]))
        x_d1.append(to_x0(d1[1].astype(bf16)))

        early, swapped, q_sum = [], [], []
        for j in (0, 1):
            s0 = d0[j] + x_d0[j * snps : (j + 1) * snps].astype(f32)
            s2 = d2[j] + x_d2[j].astype(f32)
            s2_low = d2[j][TILE:] + x_low[j * TILE : (j + 1) * TILE].astype(f32)
            low0, low1 = jnp.where(x_first, s2_low, 0.0), jnp.where(x_first, s0[TILE:], s2[TILE:])
            early.append((jnp.where(x_first, s0[:TILE], s2[:TILE]), jnp.where(first_core, low0, low1)))
            packed = jnp.concatenate(early[j], axis=0).astype(bf16)
            swapped.append(core_swap(packed))
            part = slice(j * TILE, (j + 1) * TILE)
            q_sum.append(q_near[part].astype(f32) + q_far[part].astype(f32))
        out = jnp.zeros((snps, snps), f32)

        def put(out, tile, row, col):
            return lax.dynamic_update_slice(out, tile, (row * TILE, col * WIDTH))

        late, moved = [], []
        for j in (0, 1):
            total = jnp.where(x_first, d1[j] + x_d1[j].astype(f32), z_near[j].astype(f32) + z_far[j].astype(f32))
            late.append(total)
            moved.append(perm(total[:TILE].astype(bf16), lambda xx, c, p: (xx, 1, p) if c == 0 else None))
        for j in (0, 1):
            from_other = swapped[j][TILE:].astype(f32)
            kept_low = jnp.where(first_core, late[j][TILE:], jnp.where(x_first, from_other, q_sum[j]))
            out = put(out, jnp.where(first_core, early[j][0], moved[j].astype(f32)), 0, j)
            out = put(out, jnp.where(first_core, swapped[j][:TILE].astype(f32), late[j][:TILE]), 0, 2 + j)
            out = put(out, jnp.where(first_core, from_other, late[j][TILE:]), 1, j)
            out = put(out, kept_low, 1, 2 + j)
        return out

    return on_device


def solution(mesh):
    body = make_on_device(mesh.shape["samp"], mesh.shape["snp"])

    return jax.shard_map(body, mesh=mesh, in_specs=(P("samp", "snp"),), out_specs=P("snp", "samp"), check_vma=False)
```

time: 372 us -> 160 us (0.43)
  the two profiles are of different devices: /device:TPU:0 before, /device:TPU:23 now
where the time goes in v1:
time: 160 us; the launch traced here: 159 us
  waiting for transfers between devices  69.3 us (43%)
  starting transfers between devices  54.3 us (34%)
  matrix products  18 us (11%)
  other arithmetic  13.4 us (8%)
  local copies, waits for them, and re-layouts  3.07 us (2%)
    ppermute x31, waiting for transfers between devices, perm(): return lax.ppermute(x, axes, pairs)  69.3 us
    ppermute x31, starting transfers between devices, perm(): return lax.ppermute(x, axes, pairs)  54.3 us
    dot_general x20, matrix products, dot_t(): lax.dot_general(rows, cols, (((0,), (0,)), ((), ())), preferred_element_t...  18 us
    convert_element_type x2, other arithmetic, standardized(): return jnp.where(g >= 0, (g - by[0]) * by[1], 0.0).astype(bf16)  4.22 us
  transfers between devices with their start and end apart: 31, of which 12 were waited for; matrix products, arithmetic and copies ran while one was open for 15% of the time, Pallas kernels for 0%

profile of v1, /device:TPU:23, one launch (start us, length us, event | category | flops | bytes accessed | tf_op | source)
XLA Modules:
  0.0 158.9 jit_solution(18021172646713835351)
XLA Ops:
  0.0 3.2 %convert_reduce_fusion = (f32[1024]{0:T(1024)S(1)}, f32[1024]{0:T(1024)S(1)}, f32[1024]{0:T(1024)S(1)}) fusion(f32[1024,1024]{1,0:T(8,128)} %param.1), kind=kLoop, calls=%fused_computation.2 | loop fusion | flops 7336960 | bytes 4206592 | tf_op jit(solution)/shard_map/reduce_sum | solution.py:69
  5.1 2.3 %collective-permute-done.1 = f32[3,1024]{1,0:T(4,128)S(1)} collective-permute-done((f32[3,1024]{1,0:T(4,128)S(1)}, f32[3,1024]{1,0:T(4,128)S(1)}, u32[]{:S(2)}, u32[]{:S(2)}) %collective-permute-start.1) | collective-permute-done | bytes 12320 | tf_op jit(solution)/shard_map/ppermute | solution.py:29
  9.0 2.8 %select_convert_fusion = bf16[1024,1024]{1,0:T(8,128)(2,1)S(1)} fusion(f32[1024,1024]{1,0:T(8,128)} %param.1, f32[1024]{0:T(1024)S(1)} %bitcast.55, f32[1024]{0:T(1024)S(1)} %bitcast.54), kind=kLoop, calls=%fused_computation | loop fusion | flops 5242880 | bytes 6299648 | tf_op jit(solution)/shard_map/convert_element_type | solution.py:80
  13.4 2.1 %collective-permute-start.3 = (bf16[1024,256]{1,0:T(8,128)(2,1)S(1)}, bf16[1024,256]{1,0:T(8,128)(2,1)}, u32[]{:S(2)}, u32[]{:S(2)}) collective-permute-start(bf16[1024,256]{1,0:T(8,128)(2,1)S(1)} %select_convert_fusion.1), channel_id=1, source_target_pairs={{2,0},{3,1},{4,2},{5,3},{6,4},{7,5},{10,8},{11,9},{12,10},{13,11},... | collective-permute-start | bytes 1572872 | tf_op jit(solution)/shard_map/ppermute | solution.py:29
  15.6 2.3 %collective-permute-start.4 = (bf16[1024,256]{1,0:T(8,128)(2,1)S(1)}, bf16[1024,256]{1,0:T(8,128)(2,1)}, u32[]{:S(2)}, u32[]{:S(2)}) collective-permute-start(bf16[1024,256]{1,0:T(8,128)(2,1)S(1)} %constant_dynamic-slice_fusion.3), channel_id=1, source_target_pairs={{2,8},{3,9},{4,10},{5,11},{6,12},{7,13},{10,0},{11,1},{12,2},{13,3... | collective-permute-start | bytes 1572872 | tf_op jit(solution)/shard_map/ppermute | solution.py:29
  18.2 3.9 %collective-permute-start.13 = (bf16[1024,1024]{1,0:T(8,128)(2,1)S(1)}, bf16[1024,1024]{1,0:T(8,128)(2,1)S(1)}, u32[]{:S(2)}, u32[]{:S(2)}) collective-permute-start(bf16[1024,1024]{1,0:T(8,128)(2,1)S(1)} %select_convert_fusion), channel_id=1, source_target_pairs={{0,2},{1,3},{2,4},{3,5},{4,6},{5,7},{8,10},{9,11},{10,12},{11,13},... | collective-permute-start | bytes 6291464 | tf_op jit(solution)/shard_map/ppermute | solution.py:29
  22.1 6.8 %collective-permute-done.3 = bf16[1024,256]{1,0:T(8,128)(2,1)} collective-permute-done((bf16[1024,256]{1,0:T(8,128)(2,1)S(1)}, bf16[1024,256]{1,0:T(8,128)(2,1)}, u32[]{:S(2)}, u32[]{:S(2)}) %collective-permute-start.3) | collective-permute-done | bytes 524320 | tf_op jit(solution)/shard_map/ppermute | solution.py:29
  30.5 10.0 %collective-permute-done.4 = bf16[1024,256]{1,0:T(8,128)(2,1)} collective-permute-done((bf16[1024,256]{1,0:T(8,128)(2,1)S(1)}, bf16[1024,256]{1,0:T(8,128)(2,1)}, u32[]{:S(2)}, u32[]{:S(2)}) %collective-permute-start.4) | collective-permute-done | bytes 524320 | tf_op jit(solution)/shard_map/ppermute | solution.py:29
  40.5 2.1 %collective-permute-start.9 = (bf16[1024,256]{1,0:T(8,128)(2,1)S(1)}, bf16[1024,256]{1,0:T(8,128)(2,1)S(1)}, u32[]{:S(2)}, u32[]{:S(2)}) collective-permute-start(bf16[1024,256]{1,0:T(8,128)(2,1)S(1)} %constant_dynamic-slice_fusion.2), channel_id=1, source_target_pairs={{2,0},{3,1},{4,2},{5,3},{6,4},{7,5},{10,8},{11,9},{12,10},{13,11},... | collective-permute-start | bytes 1572872 | tf_op jit(solution)/shard_map/ppermute | solution.py:29
  48.3 2.8 %collective-permute-start.14 = (bf16[1024,256]{1,0:T(8,128)(2,1)S(1)}, bf16[1024,256]{1,0:T(8,128)(2,1)S(1)}, u32[]{:S(2)}, u32[]{:S(2)}) collective-permute-start(bf16[1024,256]{1,0:T(8,128)(2,1)S(1)} %constant_dynamic-slice_fusion.1), channel_id=1, source_target_pairs={{2,8},{3,9},{4,10},{5,11},{6,12},{7,13},{10,0},{11,1},{12,2},{13,3... | collective-permute-start | bytes 1572872 | tf_op jit(solution)/shard_map/ppermute | solution.py:29
  56.6 10.5 %collective-permute-done.10 = bf16[1024,256]{1,0:T(8,128)(2,1)S(1)} collective-permute-done((bf16[1024,256]{1,0:T(8,128)(2,1)S(1)}, bf16[1024,256]{1,0:T(8,128)(2,1)S(1)}, u32[]{:S(2)}, u32[]{:S(2)}) %collective-permute-start.10) | collective-permute-done | bytes 524320 | tf_op jit(solution)/shard_map/ppermute | solution.py:29
  68.0 2.7 %collective-permute-start.25 = (bf16[1024,256]{1,0:T(8,128)(2,1)S(1)}, bf16[1024,256]{1,0:T(8,128)(2,1)S(1)}, u32[]{:S(2)}, u32[]{:S(2)}) collective-permute-start(bf16[1024,256]{1,0:T(8,128)(2,1)S(1)} %broadcast_select_fusion), channel_id=1, source_target_pairs={{0,1},{1,8},{2,3},{3,10},{4,5},{5,12},{6,7},{7,14},{8,9},{9,0},{10... | collective-permute-start | bytes 1572872 | tf_op jit(solution)/shard_map/ppermute | solution.py:29
  73.6 4.1 %collective-permute-start.7 = (bf16[2048,256]{1,0:T(8,128)(2,1)S(1)}, bf16[2048,256]{1,0:T(8,128)(2,1)S(1)}, u32[]{:S(2)}, u32[]{:S(2)}) collective-permute-start(bf16[2048,256]{1,0:T(8,128)(2,1)S(1)} %pad_maximum_fusion), channel_id=1, source_target_pairs={{16,0},{17,1},{18,2},{19,3},{20,4},{21,5},{22,6},{23,7},{24,8},{25... | collective-permute-start | bytes 3145736 | tf_op jit(solution)/shard_map/ppermute | solution.py:29
  79.4 8.5 %collective-permute-done.23 = bf16[1024,256]{1,0:T(8,128)(2,1)S(1)} collective-permute-done((bf16[1024,256]{1,0:T(8,128)(2,1)S(1)}, bf16[1024,256]{1,0:T(8,128)(2,1)S(1)}, u32[]{:S(2)}, u32[]{:S(2)}) %collective-permute-start.23) | collective-permute-done | bytes 524320 | tf_op jit(solution)/shard_map/ppermute | solution.py:29
  90.8 11.9 %collective-permute-done.8 = bf16[1024,256]{1,0:T(8,128)(2,1)S(1)} collective-permute-done((bf16[1024,256]{1,0:T(8,128)(2,1)S(1)}, bf16[1024,256]{1,0:T(8,128)(2,1)S(1)}, u32[]{:S(2)}, u32[]{:S(2)}) %collective-permute-start.8) | collective-permute-done | bytes 524320 | tf_op jit(solution)/shard_map/ppermute | solution.py:29
  112.2 1.9 %collective-permute-start.27 = (bf16[1024,256]{1,0:T(8,128)(2,1)S(1)}, bf16[1024,256]{1,0:T(8,128)(2,1)S(1)}, u32[]{:S(2)}, u32[]{:S(2)}) collective-permute-start(bf16[1024,256]{1,0:T(8,128)(2,1)S(1)} %convolution_add_fusion.1), channel_id=1, source_target_pairs={{18,16},{19,17},{20,18},{21,19},{22,20},{23,21},{26,24},{27,25},{2... | collective-permute-start | bytes 1572872 | tf_op jit(solution)/shard_map/ppermute | solution.py:29
  115.4 1.9 %collective-permute-start.16 = (bf16[1024,256]{1,0:T(8,128)(2,1)S(1)}, bf16[1024,256]{1,0:T(8,128)(2,1)S(1)}, u32[]{:S(2)}, u32[]{:S(2)}) collective-permute-start(bf16[1024,256]{1,0:T(8,128)(2,1)S(1)} %convolution_add_fusion.2), channel_id=1, source_target_pairs={{18,16},{19,17},{20,18},{21,19},{22,20},{23,21},{26,24},{27,25},{2... | collective-permute-start | bytes 1572872 | tf_op jit(solution)/shard_map/ppermute | solution.py:29
  119.5 3.6 %collective-permute-start.26 = (bf16[1024,256]{1,0:T(8,128)(2,1)S(1)}, bf16[1024,256]{1,0:T(8,128)(2,1)S(1)}, u32[]{:S(2)}, u32[]{:S(2)}) collective-permute-start(bf16[1024,256]{1,0:T(8,128)(2,1)S(1)} %convert_element_type.125), channel_id=1, source_target_pairs={{16,0},{17,1},{18,2},{19,3},{20,4},{21,5},{22,6},{23,7},{24,8},{25... | collective-permute-start | bytes 1572872 | tf_op jit(solution)/shard_map/ppermute | solution.py:29
  123.2 11.6 %collective-permute-done.16 = bf16[1024,256]{1,0:T(8,128)(2,1)S(1)} collective-permute-done((bf16[1024,256]{1,0:T(8,128)(2,1)S(1)}, bf16[1024,256]{1,0:T(8,128)(2,1)S(1)}, u32[]{:S(2)}, u32[]{:S(2)}) %collective-permute-start.16) | collective-permute-done | bytes 524320 | tf_op jit(solution)/shard_map/ppermute | solution.py:29
  134.8 4.8 %collective-permute-start.30 = (bf16[1024,256]{1,0:T(8,128)(2,1)S(1)}, bf16[1024,256]{1,0:T(8,128)(2,1)S(1)}, u32[]{:S(2)}, u32[]{:S(2)}) collective-permute-start(bf16[1024,256]{1,0:T(8,128)(2,1)S(1)} %pad_maximum_fusion.4), channel_id=1, source_target_pairs={{0,8},{1,9},{2,10},{3,11},{4,12},{5,13},{6,14},{7,15},{8,0},{9,1},... | collective-permute-start | bytes 1572872 | tf_op jit(solution)/shard_map/ppermute | solution.py:29
  139.7 2.8 %collective-permute-start.20 = (bf16[1024,256]{1,0:T(8,128)(2,1)S(1)}, bf16[1024,256]{1,0:T(8,128)(2,1)S(1)}, u32[]{:S(2)}, u32[]{:S(2)}) collective-permute-start(bf16[1024,256]{1,0:T(8,128)(2,1)S(1)} %pad_maximum_fusion.2), channel_id=1, source_target_pairs={{0,8},{1,9},{2,10},{3,11},{4,12},{5,13},{6,14},{7,15},{8,0},{9,1},... | collective-permute-start | bytes 1572872 | tf_op jit(solution)/shard_map/ppermute | solution.py:29
  151.0 2.4 %collective-permute-done.21 = bf16[1024,256]{1,0:T(8,128)(2,1)S(1)} collective-permute-done((bf16[1024,256]{1,0:T(8,128)(2,1)S(1)}, bf16[1024,256]{1,0:T(8,128)(2,1)S(1)}, u32[]{:S(2)}, u32[]{:S(2)}) %collective-permute-start.21) | collective-permute-done | bytes 524320 | tf_op jit(solution)/shard_map/ppermute | solution.py:29
  153.4 2.2 %collective-permute-done.22 = bf16[1024,256]{1,0:T(8,128)(2,1)S(1)} collective-permute-done((bf16[1024,256]{1,0:T(8,128)(2,1)S(1)}, bf16[1024,256]{1,0:T(8,128)(2,1)S(1)}, u32[]{:S(2)}, u32[]{:S(2)}) %collective-permute-start.22) | collective-permute-done | bytes 524320 | tf_op jit(solution)/shard_map/ppermute | solution.py:29
  156.0 2.0 %copy-done = f32[1024,1024]{1,0:T(8,128)} copy-done((f32[1024,1024]{1,0:T(8,128)}, f32[1024,1024]{1,0:T(8,128)S(1)}, u32[]{:S(2)}) %copy-start) | copy-done | bytes 4194328
  (111 shorter events, 48.8 us)
Async XLA Ops:
  11.9 30.8 %collective-permute-start.2 = (bf16[1024,1024]{1,0:T(8,128)(2,1)S(1)}, bf16[1024,1024]{1,0:T(8,128)(2,1)}, u32[]{:S(2)}, u32[]{:S(2)}) collective-permute-start(bf16[1024,1024]{1,0:T(8,128)(2,1)S(1)} %select_convert_fusion), channel_id=1, source_target_pairs={{0,8},{1,9},{2,10},{3,11},{4,12},{5,13},{6,14},{7,15},{8,0},{9,1},... | collective-permute-start | bytes 6291464 | tf_op jit(solution)/shard_map/ppermute | solution.py:29
  13.4 15.4 %collective-permute-start.3 = (bf16[1024,256]{1,0:T(8,128)(2,1)S(1)}, bf16[1024,256]{1,0:T(8,128)(2,1)}, u32[]{:S(2)}, u32[]{:S(2)}) collective-permute-start(bf16[1024,256]{1,0:T(8,128)(2,1)S(1)} %select_convert_fusion.1), channel_id=1, source_target_pairs={{2,0},{3,1},{4,2},{5,3},{6,4},{7,5},{10,8},{11,9},{12,10},{13,11},... | collective-permute-start | bytes 1572872 | tf_op jit(solution)/shard_map/ppermute | solution.py:29
  15.6 24.9 %collective-permute-start.4 = (bf16[1024,256]{1,0:T(8,128)(2,1)S(1)}, bf16[1024,256]{1,0:T(8,128)(2,1)}, u32[]{:S(2)}, u32[]{:S(2)}) collective-permute-start(bf16[1024,256]{1,0:T(8,128)(2,1)S(1)} %constant_dynamic-slice_fusion.3), channel_id=1, source_target_pairs={{2,8},{3,9},{4,10},{5,11},{6,12},{7,13},{10,0},{11,1},{12,2},{13,3... | collective-permute-start | bytes 1572872 | tf_op jit(solution)/shard_map/ppermute | solution.py:29
  17.9 28.7 %collective-permute-start.5 = (bf16[1024,256]{1,0:T(8,128)(2,1)S(1)}, bf16[1024,256]{1,0:T(8,128)(2,1)S(1)}, u32[]{:S(2)}, u32[]{:S(2)}) collective-permute-start(bf16[1024,256]{1,0:T(8,128)(2,1)S(1)} %constant_dynamic-slice_fusion.3), channel_id=1, source_target_pairs={{0,8},{1,9},{2,10},{3,11},{4,12},{5,13},{6,14},{7,15},{8,0},{9,1},... | collective-permute-start | bytes 1572872 | tf_op jit(solution)/shard_map/ppermute | solution.py:29
  18.2 59.5 %collective-permute-start.13 = (bf16[1024,1024]{1,0:T(8,128)(2,1)S(1)}, bf16[1024,1024]{1,0:T(8,128)(2,1)S(1)}, u32[]{:S(2)}, u32[]{:S(2)}) collective-permute-start(bf16[1024,1024]{1,0:T(8,128)(2,1)S(1)} %select_convert_fusion), channel_id=1, source_target_pairs={{0,2},{1,3},{2,4},{3,5},{4,6},{5,7},{8,10},{9,11},{10,12},{11,13},... | collective-permute-start | bytes 6291464 | tf_op jit(solution)/shard_map/ppermute | solution.py:29
  29.1 19.2 %collective-permute-start.6 = (bf16[1024,256]{1,0:T(8,128)(2,1)S(1)}, bf16[1024,256]{1,0:T(8,128)(2,1)S(1)}, u32[]{:S(2)}, u32[]{:S(2)}) collective-permute-start(bf16[1024,256]{1,0:T(8,128)(2,1)S(1)} %constant_dynamic-slice_fusion.1), channel_id=1, source_target_pairs={{0,8},{1,9},{2,10},{3,11},{4,12},{5,13},{6,14},{7,15},{8,0},{9,1},... | collective-permute-start | bytes 1572872 | tf_op jit(solution)/shard_map/ppermute | solution.py:29
  40.5 15.4 %collective-permute-start.9 = (bf16[1024,256]{1,0:T(8,128)(2,1)S(1)}, bf16[1024,256]{1,0:T(8,128)(2,1)S(1)}, u32[]{:S(2)}, u32[]{:S(2)}) collective-permute-start(bf16[1024,256]{1,0:T(8,128)(2,1)S(1)} %constant_dynamic-slice_fusion.2), channel_id=1, source_target_pairs={{2,0},{3,1},{4,2},{5,3},{6,4},{7,5},{10,8},{11,9},{12,10},{13,11},... | collective-permute-start | bytes 1572872 | tf_op jit(solution)/shard_map/ppermute | solution.py:29
  42.6 13.3 %collective-permute-start.11 = (bf16[1024,256]{1,0:T(8,128)(2,1)S(1)}, bf16[1024,256]{1,0:T(8,128)(2,1)S(1)}, u32[]{:S(2)}, u32[]{:S(2)}) collective-permute-start(bf16[1024,256]{1,0:T(8,128)(2,1)S(1)} %broadcast_select_fusion.2), channel_id=1, source_target_pairs={{0,1},{1,8},{2,3},{3,10},{4,5},{5,12},{6,7},{7,14},{8,9},{9,0},{10... | collective-permute-start | bytes 1572872 | tf_op jit(solution)/shard_map/ppermute | solution.py:29
  46.7 20.5 %collective-permute-start.10 = (bf16[1024,256]{1,0:T(8,128)(2,1)S(1)}, bf16[1024,256]{1,0:T(8,128)(2,1)S(1)}, u32[]{:S(2)}, u32[]{:S(2)}) collective-permute-start(bf16[1024,256]{1,0:T(8,128)(2,1)S(1)} %broadcast_select_fusion.3), channel_id=1, source_target_pairs={{0,1},{1,0},{2,3},{3,2},{4,5},{5,4},{6,7},{7,6},{8,9},{9,8},{10,11... | collective-permute-start | bytes 1572872 | tf_op jit(solution)/shard_map/ppermute | solution.py:29
  48.3 19.6 %collective-permute-start.14 = (bf16[1024,256]{1,0:T(8,128)(2,1)S(1)}, bf16[1024,256]{1,0:T(8,128)(2,1)S(1)}, u32[]{:S(2)}, u32[]{:S(2)}) collective-permute-start(bf16[1024,256]{1,0:T(8,128)(2,1)S(1)} %constant_dynamic-slice_fusion.1), channel_id=1, source_target_pairs={{2,8},{3,9},{4,10},{5,11},{6,12},{7,13},{10,0},{11,1},{12,2},{13,3... | collective-permute-start | bytes 1572872 | tf_op jit(solution)/shard_map/ppermute | solution.py:29
  68.0 21.3 %collective-permute-start.25 = (bf16[1024,256]{1,0:T(8,128)(2,1)S(1)}, bf16[1024,256]{1,0:T(8,128)(2,1)S(1)}, u32[]{:S(2)}, u32[]{:S(2)}) collective-permute-start(bf16[1024,256]{1,0:T(8,128)(2,1)S(1)} %broadcast_select_fusion), channel_id=1, source_target_pairs={{0,1},{1,8},{2,3},{3,10},{4,5},{5,12},{6,7},{7,14},{8,9},{9,0},{10... | collective-permute-start | bytes 1572872 | tf_op jit(solution)/shard_map/ppermute | solution.py:29
  72.2 15.7 %collective-permute-start.23 = (bf16[1024,256]{1,0:T(8,128)(2,1)S(1)}, bf16[1024,256]{1,0:T(8,128)(2,1)S(1)}, u32[]{:S(2)}, u32[]{:S(2)}) collective-permute-start(bf16[1024,256]{1,0:T(8,128)(2,1)S(1)} %convert_element_type.123), channel_id=1, source_target_pairs={{0,16},{1,17},{2,18},{3,19},{4,20},{5,21},{6,22},{7,23},{8,24},{9,... | collective-permute-start | bytes 1572872 | tf_op jit(solution)/shard_map/ppermute | solution.py:29
  73.6 30.5 %collective-permute-start.7 = (bf16[2048,256]{1,0:T(8,128)(2,1)S(1)}, bf16[2048,256]{1,0:T(8,128)(2,1)S(1)}, u32[]{:S(2)}, u32[]{:S(2)}) collective-permute-start(bf16[2048,256]{1,0:T(8,128)(2,1)S(1)} %pad_maximum_fusion), channel_id=1, source_target_pairs={{16,0},{17,1},{18,2},{19,3},{20,4},{21,5},{22,6},{23,7},{24,8},{25... | collective-permute-start | bytes 3145736 | tf_op jit(solution)/shard_map/ppermute | solution.py:29
  77.7 27.2 %collective-permute-start.15 = (bf16[1024,1024]{1,0:T(8,128)(2,1)S(1)}, bf16[1024,1024]{1,0:T(8,128)(2,1)S(1)}, u32[]{:S(2)}, u32[]{:S(2)}) collective-permute-start(bf16[1024,1024]{1,0:T(8,128)(2,1)S(1)} %collective-permute-done.13), channel_id=1, source_target_pairs={{0,8},{1,9},{2,10},{3,11},{4,12},{5,13},{6,14},{7,15},{8,0},{9,1},... | collective-permute-start | bytes 6291464 | tf_op jit(solution)/shard_map/ppermute | solution.py:29
  78.4 33.0 %collective-permute-start.24 = (bf16[1024,256]{1,0:T(8,128)(2,1)S(1)}, bf16[1024,256]{1,0:T(8,128)(2,1)S(1)}, u32[]{:S(2)}, u32[]{:S(2)}) collective-permute-start(bf16[1024,256]{1,0:T(8,128)(2,1)S(1)} %broadcast_select_fusion.1), channel_id=1, source_target_pairs={{0,1},{1,0},{2,3},{3,2},{4,5},{5,4},{6,7},{7,6},{8,9},{9,8},{10,11... | collective-permute-start | bytes 1572872 | tf_op jit(solution)/shard_map/ppermute | solution.py:29
  87.9 14.8 %collective-permute-start.8 = (bf16[1024,256]{1,0:T(8,128)(2,1)S(1)}, bf16[1024,256]{1,0:T(8,128)(2,1)S(1)}, u32[]{:S(2)}, u32[]{:S(2)}) collective-permute-start(bf16[1024,256]{1,0:T(8,128)(2,1)S(1)} %convert_element_type.108), channel_id=1, source_target_pairs={{0,16},{1,17},{2,18},{3,19},{4,20},{5,21},{6,22},{7,23},{8,24},{9,... | collective-permute-start | bytes 1572872 | tf_op jit(solution)/shard_map/ppermute | solution.py:29
  89.3 15.1 %collective-permute-start.19 = (bf16[1024,256]{1,0:T(8,128)(2,1)S(1)}, bf16[1024,256]{1,0:T(8,128)(2,1)S(1)}, u32[]{:S(2)}, u32[]{:S(2)}) collective-permute-start(bf16[1024,256]{1,0:T(8,128)(2,1)S(1)} %pad_maximum_fusion.1), channel_id=1, source_target_pairs={{16,0},{17,1},{18,2},{19,3},{20,4},{21,5},{22,6},{23,7}} | collective-permute-start | bytes 1572872 | tf_op jit(solution)/shard_map/ppermute | solution.py:29
  102.7 16.8 %collective-permute-start.12 = (bf16[1024,256]{1,0:T(8,128)(2,1)S(1)}, bf16[1024,256]{1,0:T(8,128)(2,1)S(1)}, u32[]{:S(2)}, u32[]{:S(2)}) collective-permute-start(bf16[1024,256]{1,0:T(8,128)(2,1)S(1)} %convert_element_type.110), channel_id=1, source_target_pairs={{16,0},{17,1},{18,2},{19,3},{20,4},{21,5},{22,6},{23,7},{24,8},{25... | collective-permute-start | bytes 1572872 | tf_op jit(solution)/shard_map/ppermute | solution.py:29
  112.2 32.0 %collective-permute-start.27 = (bf16[1024,256]{1,0:T(8,128)(2,1)S(1)}, bf16[1024,256]{1,0:T(8,128)(2,1)S(1)}, u32[]{:S(2)}, u32[]{:S(2)}) collective-permute-start(bf16[1024,256]{1,0:T(8,128)(2,1)S(1)} %convolution_add_fusion.1), channel_id=1, source_target_pairs={{18,16},{19,17},{20,18},{21,19},{22,20},{23,21},{26,24},{27,25},{2... | collective-permute-start | bytes 1572872 | tf_op jit(solution)/shard_map/ppermute | solution.py:29
  114.1 31.4 %collective-permute-start.28 = (bf16[1024,256]{1,0:T(8,128)(2,1)S(1)}, bf16[1024,256]{1,0:T(8,128)(2,1)S(1)}, u32[]{:S(2)}, u32[]{:S(2)}) collective-permute-start(bf16[1024,256]{1,0:T(8,128)(2,1)S(1)} %convolution_add_fusion.1), channel_id=1, source_target_pairs={{2,16},{3,17},{4,18},{5,19},{6,20},{7,21},{10,24},{11,25},{12,26},... | collective-permute-start | bytes 1572872 | tf_op jit(solution)/shard_map/ppermute | solution.py:29
  115.4 19.4 %collective-permute-start.16 = (bf16[1024,256]{1,0:T(8,128)(2,1)S(1)}, bf16[1024,256]{1,0:T(8,128)(2,1)S(1)}, u32[]{:S(2)}, u32[]{:S(2)}) collective-permute-start(bf16[1024,256]{1,0:T(8,128)(2,1)S(1)} %convolution_add_fusion.2), channel_id=1, source_target_pairs={{18,16},{19,17},{20,18},{21,19},{22,20},{23,21},{26,24},{27,25},{2... | collective-permute-start | bytes 1572872 | tf_op jit(solution)/shard_map/ppermute | solution.py:29
  117.3 22.3 %collective-permute-start.17 = (bf16[1024,256]{1,0:T(8,128)(2,1)S(1)}, bf16[1024,256]{1,0:T(8,128)(2,1)S(1)}, u32[]{:S(2)}, u32[]{:S(2)}) collective-permute-start(bf16[1024,256]{1,0:T(8,128)(2,1)S(1)} %convolution_add_fusion.2), channel_id=1, source_target_pairs={{2,16},{3,17},{4,18},{5,19},{6,20},{7,21},{10,24},{11,25},{12,26},... | collective-permute-start | bytes 1572872 | tf_op jit(solution)/shard_map/ppermute | solution.py:29
  119.5 23.4 %collective-permute-start.26 = (bf16[1024,256]{1,0:T(8,128)(2,1)S(1)}, bf16[1024,256]{1,0:T(8,128)(2,1)S(1)}, u32[]{:S(2)}, u32[]{:S(2)}) collective-permute-start(bf16[1024,256]{1,0:T(8,128)(2,1)S(1)} %convert_element_type.125), channel_id=1, source_target_pairs={{16,0},{17,1},{18,2},{19,3},{20,4},{21,5},{22,6},{23,7},{24,8},{25... | collective-permute-start | bytes 1572872 | tf_op jit(solution)/shard_map/ppermute | solution.py:29
  134.8 21.0 %collective-permute-start.30 = (bf16[1024,256]{1,0:T(8,128)(2,1)S(1)}, bf16[1024,256]{1,0:T(8,128)(2,1)S(1)}, u32[]{:S(2)}, u32[]{:S(2)}) collective-permute-start(bf16[1024,256]{1,0:T(8,128)(2,1)S(1)} %pad_maximum_fusion.4), channel_id=1, source_target_pairs={{0,8},{1,9},{2,10},{3,11},{4,12},{5,13},{6,14},{7,15},{8,0},{9,1},... | collective-permute-start | bytes 1572872 | tf_op jit(solution)/shard_map/ppermute | solution.py:29
  (8 other events, 49.5 us)

commit v2 on v1

v2 whole, which is shorter than its diff:
```python
import functools

import jax
import jax.numpy as jnp
from jax import lax
from jax.experimental import pallas as pl
from jax.experimental.pallas import tpu as pltpu
from jax.sharding import PartitionSpec as P


TILE = 512
BAND = 4096
WIDTH = TILE // 2


def dot_t(rows, cols):
    return lax.dot_general(rows, cols, (((0,), (0,)), ((), ())), preferred_element_type=jnp.float32)


def merge_body(part, core_ref, keep_top, keep_low, got_top, got_low, *refs):
    out_ref, buffer, wide, sems = refs[-4:]
    core = core_ref[0]

    def put(k, source, row, col):
        start = pl.multiple_of((2 * col + part) * WIDTH, WIDTH)
        return pltpu.make_async_copy(source, out_ref.at[pl.ds(row * TILE, TILE), pl.ds(start, WIDTH)], sems.at[k])

    fetch = pltpu.make_async_copy(got_top, buffer, sems.at[4])
    fetch.start()
    copies = [put(0, keep_top, 0, core), put(1, keep_low, 1, 1 - core), put(2, got_low, 1, core)]
    for copy in copies:
        copy.start()
    fetch.wait()
    wide[...] = buffer[...].astype(jnp.float32)
    last = put(3, wide, 0, 1 - core)
    last.start()
    for copy in copies:
        copy.wait()
    last.wait()


def merge(part, core, tiles, into, columns):
    vmem, anywhere = pl.BlockSpec(memory_space=pltpu.VMEM), pl.BlockSpec(memory_space=pl.ANY)
    tiles = tiles + (() if into is None else (into,))
    return pl.pallas_call(
        functools.partial(merge_body, part),
        grid_spec=pltpu.PrefetchScalarGridSpec(
            num_scalar_prefetch=1,
            grid=(1,),
            in_specs=[vmem, vmem, anywhere, vmem] + [anywhere] * (len(tiles) - 4),
            out_specs=anywhere,
            scratch_shapes=[
                pltpu.VMEM((TILE, WIDTH), jnp.bfloat16),
                pltpu.VMEM((TILE, WIDTH), jnp.float32),
                pltpu.SemaphoreType.DMA((5,)),
            ],
        ),
        out_shape=jax.ShapeDtypeStruct((2 * TILE, columns), jnp.float32),
        input_output_aliases={} if into is None else {5: 0},
        compiler_params=pltpu.CompilerParams(vmem_limit_bytes=8 * 2**20),
        cost_estimate=pl.CostEstimate(flops=TILE * columns, bytes_accessed=4 * TILE * columns, transcendentals=0),
    )(core, *tiles)


def make_on_device(samp_size, snp_size):
    axes = ("samp", "snp")

    def perm(x, move):
        pairs = []
        for samp in range(samp_size):
            for p in range(snp_size):
                target = move(samp // 2, samp % 2, p)
                if target is None:
                    continue
                tx, tc, tp = target
                if 0 <= tp < snp_size:
                    pairs.append((samp * snp_size + p, (tx * 2 + tc) * snp_size + tp))
        return lax.ppermute(x, axes, pairs)

    def core_swap(x):
        return perm(x, lambda xx, c, p: (xx, 1 - c, p))

    def x_swap(x):
        return perm(x, lambda xx, c, p: (1 - xx, c, p))

    def to_x0(x):
        return perm(x, lambda xx, c, p: (0, c, p) if xx == 1 else None)

    def to_x1(x):
        return perm(x, lambda xx, c, p: (1, c, p) if xx == 0 else None)

    def relay(c, p, crossed):
        return (c, p + 1) if p % 2 == 0 else (1 - c if crossed else c, p - 1)

    def on_device(genotypes):
        _, snps = genotypes.shape
        assert samp_size == 4 and snp_size % 2 == 0
        assert snps == 2 * TILE and BAND == 4 * snps
        bf16, f32 = jnp.bfloat16, jnp.float32
        samp = lax.axis_index("samp")
        xx, core = samp // 2, samp % 2
        x_first, first_core = xx == 0, core == 0
        even = (lax.axis_index("snp") % 2) == 0

        last = [None]

        def after(x):
            return x if last[0] is None else lax.optimization_barrier((x, last[0]))[0]

        def step(make, *args):
            args = (after(args[0]), *args[1:])
            last[0] = make(*args)
            last[0] = lax.optimization_barrier(last[0])
            return last[0]

        present = (genotypes >= 0).astype(f32)
        dosage = genotypes * present
        stats = jnp.stack([jnp.sum(present, axis=0), jnp.sum(dosage, axis=0), jnp.sum(dosage * dosage, axis=0)])
        stats = stats + core_swap(stats)
        stats = stats + x_swap(stats)
        average = stats[1] / stats[0]
        factor = lax.rsqrt(stats[0] * (stats[2] / stats[0] - average * average))
        scale = lax.optimization_barrier(jnp.stack([average, factor]))

        def columns(x, start, width=WIDTH):
            return lax.dynamic_slice_in_dim(x, start, width, 1)

        def standardized(by, g):
            return jnp.where(g >= 0, (g - by[0]) * by[1], 0.0).astype(bf16)

        def staged(x):
            return jnp.maximum(x, jnp.finfo(bf16).min)

        def send_same(j):
            return perm(keep[j], lambda xx, c, p: (xx, c, p - 2))

        def send_cross(j):
            return perm(give[j], lambda xx, c, p: (xx, 1 - c, p - 2))

        def relay_same(j):
            payload = step(lambda e: jnp.where(e, above[j][0], keep[j]), even)
            return perm(payload, lambda xx, c, p: (xx, *relay(c, p, False)))

        def relay_cross(j):
            payload = step(lambda e: jnp.where(e, above[j][1], give[j]), even)
            return perm(payload, lambda xx, c, p: (xx, *relay(c, p, True)))

        def pair(rows, cols):
            return step(lambda r: (dot_t(r, cols[0]) + dot_t(rows[1], cols[1])).astype(bf16), rows[0])

        keep_start, give_start = core * TILE, (1 - core) * TILE
        keep = [step(lambda by: standardized(columns(by, keep_start), columns(genotypes, keep_start)), scale)]
        above = [[send_same(0)]]
        mine = step(standardized, scale, genotypes)
        up = perm(mine, lambda xx, c, p: (xx, c, p + 2))
        theirs = core_swap(mine)
        give = [step(columns, mine, give_start)]
        above[0].append(send_cross(0))
        across = core_swap(step(lambda m: columns(m, give_start, TILE), mine))
        nexts = [[relay_same(0)]]
        keep.append(step(columns, mine, keep_start + WIDTH))
        above.append([send_same(1)])
        give.append(step(columns, mine, give_start + WIDTH))
        above[1].append(send_cross(1))
        rows = (mine, step(staged, theirs))
        own = columns(after(mine), keep_start, TILE)
        d0 = pair(rows, (own, across))
        nexts[0].append(relay_cross(0))
        x_d0 = to_x0(d0)


        d2 = [pair(rows, above[0])]
        x_d2 = to_x1(d2[0])
        nexts.append([relay_same(1)])
        d1 = [pair(rows, nexts[0])]
        x_d1 = [to_x0(jnp.concatenate([d1[0], d2[0][TILE:]], axis=0))]
        nexts[1].append(relay_cross(1))
        d2.append(pair(rows, above[1]))
        x_top = to_x1(d2[1][:TILE])
        x_low = perm(d2[1][TILE:], lambda xx, c, p: (1, 1, p) if (xx, c) == (0, 1) else None)
        other_up = core_swap(up)
        below = (step(staged, up), step(staged, other_up))
        z_near, z_far = [], []

        def send_d3(j):
            part = pair(below, nexts[j])
            z_far.append(perm(part, lambda xx, c, p: (1, c, p - 2) if xx == 0 else None))
            z_near.append(perm(part, lambda xx, c, p: (1, c, p - 2) if xx == 1 else None))

        send_d3(0)
        below_low = (below[0][:, TILE:], below[1][:, TILE:])
        d4 = jnp.concatenate([pair(below_low, a) for a in above], axis=0)
        q_near = perm(d4, lambda xx, c, p: (1, 1, p - 2) if (xx, c) == (1, 0) else None)
        q_far = perm(d4, lambda xx, c, p: (1, 1, p - 2) if (xx, c) == (0, 0) else None)
        nexts[1] = [step(staged, n) for n in nexts[1]]
        d1.append(pair(rows, nexts[1]))
        part = jnp.concatenate([d1[1], d2[1][TILE:]], axis=0)
        x_d1.append(to_x0(part))
        send_d3(1)

        core_arg = core[None].astype(jnp.int32)
        out = None
        for j in (0, 1):
            cols = slice(j * WIDTH, (j + 1) * WIDTH)
            s0 = d0[:, cols].astype(f32) + x_d0[:, cols].astype(f32)
            upper, lower = (x_d2[:TILE], x_d2[TILE:]) if j == 0 else (x_top, x_low)
            s2_top = d2[j][:TILE].astype(f32) + upper.astype(f32)
            s2_low = d2[j][TILE:].astype(f32) + jnp.where(x_first, x_d1[j][snps:], lower).astype(f32)
            early_top = jnp.where(x_first, s0[:TILE], s2_top)
            early_low = jnp.where(first_core | ~x_first, s2_low, s0[TILE:])
            late = jnp.where(
                x_first,
                d1[j].astype(f32) + x_d1[j][:snps].astype(f32),
                z_near[j].astype(f32) + z_far[j].astype(f32),
            )
            part = slice(j * TILE, (j + 1) * TILE)
            q_sum = q_near[part].astype(f32) + q_far[part].astype(f32)
            give_top = jnp.where(first_core, late[:TILE], early_top).astype(bf16)
            keep_top = jnp.where(first_core, early_top, late[:TILE])
            send = jnp.concatenate([give_top, early_low.astype(bf16)], axis=0)
            got = core_swap(send)
            got_low = jnp.where(x_first | first_core, got[TILE:].astype(f32), q_sum)
            out = merge(j, core_arg, (keep_top, late[TILE:], got[:TILE], got_low), out, snps)
        return out

    return on_device


def solution(mesh):
    body = make_on_device(mesh.shape["samp"], mesh.shape["snp"])

    return jax.shard_map(body, mesh=mesh, in_specs=(P("samp", "snp"),), out_specs=P("snp", "samp"), check_vma=False)
```

time: 160 us -> 144 us (0.900)
  the two profiles are of different devices: /device:TPU:23 before, /device:TPU:0 now
where the time goes in v2:
time: 144 us; the launch traced here: 143 us
  waiting for transfers between devices  75.7 us (53%)
  starting transfers between devices  37.7 us (26%)
  matrix products  13.5 us (9%)
  other arithmetic  11.9 us (8%)
  Pallas kernels  2.75 us (2%)
    ppermute x28, waiting for transfers between devices, perm(): return lax.ppermute(x, axes, pairs)  75.7 us
    ppermute x28, starting transfers between devices, perm(): return lax.ppermute(x, axes, pairs)  37.7 us
    dot_general x18, matrix products, dot_t(): lax.dot_general(rows, cols, (((0,), (0,)), ((), ())), preferred_element_t...  13.5 us
    convert_element_type x2, other arithmetic, standardized(): return jnp.where(g >= 0, (g - by[0]) * by[1], 0.0).astype(bf16)  4.22 us
    reduce_sum x1, other arithmetic, on_device(): jnp.sum(present, axis=0)  3.16 us
  transfers between devices with their start and end apart: 28, of which 11 were waited for; matrix products, arithmetic and copies ran while one was open for 13% of the time, Pallas kernels for 0%

profile of v2, /device:TPU:0, one launch (start us, length us, event | category | flops | bytes accessed | tf_op | source)
XLA Modules:
  0.0 143.1 jit_solution(3719247939389102691)
XLA Ops:
  0.0 3.2 %convert_reduce_fusion = (f32[1024]{0:T(1024)S(1)}, f32[1024]{0:T(1024)S(1)}, f32[1024]{0:T(1024)S(1)}) fusion(f32[1024,1024]{1,0:T(8,128)} %param.1), kind=kLoop, calls=%fused_computation.2 | loop fusion | flops 7336960 | bytes 4206592 | tf_op jit(solution)/shard_map/reduce_sum | solution.py:118
  4.6 2.9 %collective-permute-start.1 = (f32[3,1024]{1,0:T(4,128)S(1)}, f32[3,1024]{1,0:T(4,128)S(1)}, u32[]{:S(2)}, u32[]{:S(2)}) collective-permute-start(f32[3,1024]{1,0:T(4,128)S(1)} %fusion.20), channel_id=1, source_target_pairs={{0,16},{1,17},{2,18},{3,19},{4,20},{5,21},{6,22},{7,23},{8,24},{9,... | collective-permute-start | bytes 36872 | tf_op jit(solution)/shard_map/ppermute | solution.py:78
  7.5 1.7 %collective-permute-done.1 = f32[3,1024]{1,0:T(4,128)S(1)} collective-permute-done((f32[3,1024]{1,0:T(4,128)S(1)}, f32[3,1024]{1,0:T(4,128)S(1)}, u32[]{:S(2)}, u32[]{:S(2)}) %collective-permute-start.1) | collective-permute-done | bytes 12320 | tf_op jit(solution)/shard_map/ppermute | solution.py:78
  9.4 1.4 select_convert_fusion.1
  10.8 2.8 %select_convert_fusion = bf16[1024,1024]{1,0:T(8,128)(2,1)S(1)} fusion(f32[1024,1024]{1,0:T(8,128)} %param.1, f32[1024]{0:T(1024)S(1)} %bitcast.51, f32[1024]{0:T(1024)S(1)} %bitcast.50), kind=kLoop, calls=%fused_computation | loop fusion | flops 5242880 | bytes 6299648 | tf_op jit(solution)/shard_map/convert_element_type | solution.py:129
  15.1 4.8 %collective-permute-start.14 = (bf16[1024,1024]{1,0:T(8,128)(2,1)S(1)}, bf16[1024,1024]{1,0:T(8,128)(2,1)S(1)}, u32[]{:S(2)}, u32[]{:S(2)}) collective-permute-start(bf16[1024,1024]{1,0:T(8,128)(2,1)S(1)} %select_convert_fusion), channel_id=1, source_target_pairs={{0,2},{1,3},{2,4},{3,5},{4,6},{5,7},{8,10},{9,11},{10,12},{11,13},... | collective-permute-start | bytes 6291464 | tf_op jit(solution)/shard_map/ppermute | solution.py:78
  21.6 8.9 %collective-permute-done.3 = bf16[1024,256]{1,0:T(8,128)(2,1)S(1)} collective-permute-done((bf16[1024,256]{1,0:T(8,128)(2,1)S(1)}, bf16[1024,256]{1,0:T(8,128)(2,1)S(1)}, u32[]{:S(2)}, u32[]{:S(2)}) %collective-permute-start.3) | collective-permute-done | bytes 524320 | tf_op jit(solution)/shard_map/ppermute | solution.py:78
  33.3 1.8 %broadcast_maximum_fusion.2 = bf16[1024,1024]{1,0:T(8,128)(2,1)S(1)} fusion(bf16[1024,1024]{1,0:T(8,128)(2,1)} %collective-permute-done.2), kind=kLoop, calls=%fused_computation.29 | loop fusion | flops 1048576 | bytes 4194304 | tf_op jit(solution)/shard_map/max | solution.py:132
  36.4 2.0 %collective-permute-start.8 = (bf16[1024,256]{1,0:T(8,128)(2,1)S(1)}, bf16[1024,256]{1,0:T(8,128)(2,1)S(1)}, u32[]{:S(2)}, u32[]{:S(2)}) collective-permute-start(bf16[1024,256]{1,0:T(8,128)(2,1)S(1)} %broadcast_select_fusion.3), channel_id=1, source_target_pairs={{0,1},{1,0},{2,3},{3,2},{4,5},{5,4},{6,7},{7,6},{8,9},{9,8},{10,11... | collective-permute-start | bytes 1572872 | tf_op jit(solution)/shard_map/ppermute | solution.py:78
  39.7 1.6 %collective-permute-done.6 = bf16[1024,256]{1,0:T(8,128)(2,1)S(1)} collective-permute-done((bf16[1024,256]{1,0:T(8,128)(2,1)S(1)}, bf16[1024,256]{1,0:T(8,128)(2,1)S(1)}, u32[]{:S(2)}, u32[]{:S(2)}) %collective-permute-start.6) | collective-permute-done | bytes 524320 | tf_op jit(solution)/shard_map/ppermute | solution.py:78
  41.4 1.4 %collective-permute-start.9 = (bf16[1024,256]{1,0:T(8,128)(2,1)S(1)}, bf16[1024,256]{1,0:T(8,128)(2,1)S(1)}, u32[]{:S(2)}, u32[]{:S(2)}) collective-permute-start(bf16[1024,256]{1,0:T(8,128)(2,1)S(1)} %broadcast_select_fusion.2), channel_id=1, source_target_pairs={{0,1},{1,8},{2,3},{3,10},{4,5},{5,12},{6,7},{7,14},{8,9},{9,0},{10... | collective-permute-start | bytes 1572872 | tf_op jit(solution)/shard_map/ppermute | solution.py:78
  44.3 8.6 %collective-permute-done.7 = bf16[1024,256]{1,0:T(8,128)(2,1)S(1)} collective-permute-done((bf16[1024,256]{1,0:T(8,128)(2,1)S(1)}, bf16[1024,256]{1,0:T(8,128)(2,1)S(1)}, u32[]{:S(2)}, u32[]{:S(2)}) %collective-permute-start.7) | collective-permute-done | bytes 524320 | tf_op jit(solution)/shard_map/ppermute | solution.py:78
  53.0 2.0 %collective-permute-start.13 = (bf16[1024,256]{1,0:T(8,128)(2,1)S(1)}, bf16[1024,256]{1,0:T(8,128)(2,1)S(1)}, u32[]{:S(2)}, u32[]{:S(2)}) collective-permute-start(bf16[1024,256]{1,0:T(8,128)(2,1)S(1)} %broadcast_select_fusion.1), channel_id=1, source_target_pairs={{0,1},{1,0},{2,3},{3,2},{4,5},{5,4},{6,7},{7,6},{8,9},{9,8},{10,11... | collective-permute-start | bytes 1572872 | tf_op jit(solution)/shard_map/ppermute | solution.py:78
  55.1 8.7 %collective-permute-done.10 = bf16[1024,256]{1,0:T(8,128)(2,1)S(1)} collective-permute-done((bf16[1024,256]{1,0:T(8,128)(2,1)S(1)}, bf16[1024,256]{1,0:T(8,128)(2,1)S(1)}, u32[]{:S(2)}, u32[]{:S(2)}) %collective-permute-start.10) | collective-permute-done | bytes 524320 | tf_op jit(solution)/shard_map/ppermute | solution.py:78
  65.8 4.6 %collective-permute-start.23 = (bf16[1024,256]{1,0:T(8,128)(2,1)S(1)}, bf16[1024,256]{1,0:T(8,128)(2,1)S(1)}, u32[]{:S(2)}, u32[]{:S(2)}) collective-permute-start(bf16[1024,256]{1,0:T(8,128)(2,1)S(1)} %fusion), channel_id=1, source_target_pairs={{0,16},{1,17},{2,18},{3,19},{4,20},{5,21},{6,22},{7,23},{8,24},{9,... | collective-permute-start | bytes 1572872 | tf_op jit(solution)/shard_map/ppermute | solution.py:78
  72.2 1.5 %collective-permute-start.12 = (bf16[1024,256]{1,0:T(8,128)(2,1)S(1)}, bf16[1024,256]{1,0:T(8,128)(2,1)S(1)}, u32[]{:S(2)}, u32[]{:S(2)}) collective-permute-start(bf16[1024,256]{1,0:T(8,128)(2,1)S(1)} %broadcast_select_fusion), channel_id=1, source_target_pairs={{0,1},{1,8},{2,3},{3,10},{4,5},{5,12},{6,7},{7,14},{8,9},{9,0},{10... | collective-permute-start | bytes 1572872 | tf_op jit(solution)/shard_map/ppermute | solution.py:78
  74.8 16.2 %collective-permute-done.5 = bf16[1024,512]{1,0:T(8,128)(2,1)S(1)} collective-permute-done((bf16[1024,512]{1,0:T(8,128)(2,1)S(1)}, bf16[1024,512]{1,0:T(8,128)(2,1)S(1)}, u32[]{:S(2)}, u32[]{:S(2)}) %collective-permute-start.5) | collective-permute-done | bytes 1048608 | tf_op jit(solution)/shard_map/ppermute | solution.py:78
  91.0 1.5 %collective-permute-start.24 = (bf16[1536,256]{1,0:T(8,128)(2,1)S(1)}, bf16[1536,256]{1,0:T(8,128)(2,1)S(1)}, u32[]{:S(2)}, u32[]{:S(2)}) collective-permute-start(bf16[1536,256]{1,0:T(8,128)(2,1)S(1)} %pad_maximum_fusion.1), channel_id=1, source_target_pairs={{16,0},{17,1},{18,2},{19,3},{20,4},{21,5},{22,6},{23,7},{24,8},{25... | collective-permute-start | bytes 2359304 | tf_op jit(solution)/shard_map/ppermute | solution.py:78
  102.4 11.0 %collective-permute-done.24 = bf16[1536,256]{1,0:T(8,128)(2,1)S(1)} collective-permute-done((bf16[1536,256]{1,0:T(8,128)(2,1)S(1)}, bf16[1536,256]{1,0:T(8,128)(2,1)S(1)}, u32[]{:S(2)}, u32[]{:S(2)}) %collective-permute-start.24) | collective-permute-done | bytes 786464 | tf_op jit(solution)/shard_map/ppermute | solution.py:78
  115.7 3.3 %collective-permute-start.11 = (bf16[512,256]{1,0:T(8,128)(2,1)S(1)}, bf16[512,256]{1,0:T(8,128)(2,1)S(1)}, u32[]{:S(2)}, u32[]{:S(2)}) collective-permute-start(bf16[512,256]{1,0:T(8,128)(2,1)S(1)} %get-tuple-element.68), channel_id=1, source_target_pairs={{0,16},{1,17},{2,18},{3,19},{4,20},{5,21},{6,22},{7,23},{8,24},{9,... | collective-permute-start | bytes 786440 | tf_op jit(solution)/shard_map/ppermute | solution.py:78
  120.8 7.9 %collective-permute-done.16 = bf16[1536,256]{1,0:T(8,128)(2,1)S(1)} collective-permute-done((bf16[1536,256]{1,0:T(8,128)(2,1)S(1)}, bf16[1536,256]{1,0:T(8,128)(2,1)S(1)}, u32[]{:S(2)}, u32[]{:S(2)}) %collective-permute-start.16) | collective-permute-done | bytes 786464 | tf_op jit(solution)/shard_map/ppermute | solution.py:78
  128.9 8.7 %collective-permute-done.11 = bf16[512,256]{1,0:T(8,128)(2,1)S(1)} collective-permute-done((bf16[512,256]{1,0:T(8,128)(2,1)S(1)}, bf16[512,256]{1,0:T(8,128)(2,1)S(1)}, u32[]{:S(2)}, u32[]{:S(2)}) %collective-permute-start.11) | collective-permute-done | bytes 262176 | tf_op jit(solution)/shard_map/ppermute | solution.py:78
  138.4 1.5 %collective-permute-done.20 = bf16[1024,256]{1,0:T(8,128)(2,1)S(1)} collective-permute-done((bf16[1024,256]{1,0:T(8,128)(2,1)S(1)}, bf16[1024,256]{1,0:T(8,128)(2,1)S(1)}, u32[]{:S(2)}, u32[]{:S(2)}) %collective-permute-start.20) | collective-permute-done | bytes 524320 | tf_op jit(solution)/shard_map/ppermute | solution.py:78
  141.5 1.4 shard_map.18
  (93 shorter events, 32.8 us)
Async XLA Ops:
  13.6 18.4 %collective-permute-start.2 = (bf16[1024,1024]{1,0:T(8,128)(2,1)S(1)}, bf16[1024,1024]{1,0:T(8,128)(2,1)}, u32[]{:S(2)}, u32[]{:S(2)}) collective-permute-start(bf16[1024,1024]{1,0:T(8,128)(2,1)S(1)} %select_convert_fusion), channel_id=1, source_target_pairs={{0,8},{1,9},{2,10},{3,11},{4,12},{5,13},{6,14},{7,15},{8,0},{9,1},... | collective-permute-start | bytes 6291464 | tf_op jit(solution)/shard_map/ppermute | solution.py:78
  13.7 16.8 %collective-permute-start.3 = (bf16[1024,256]{1,0:T(8,128)(2,1)S(1)}, bf16[1024,256]{1,0:T(8,128)(2,1)S(1)}, u32[]{:S(2)}, u32[]{:S(2)}) collective-permute-start(bf16[1024,256]{1,0:T(8,128)(2,1)S(1)} %select_convert_fusion.1), channel_id=1, source_target_pairs={{2,0},{3,1},{4,2},{5,3},{6,4},{7,5},{10,8},{11,9},{12,10},{13,11},... | collective-permute-start | bytes 1572872 | tf_op jit(solution)/shard_map/ppermute | solution.py:78
  15.1 50.8 %collective-permute-start.14 = (bf16[1024,1024]{1,0:T(8,128)(2,1)S(1)}, bf16[1024,1024]{1,0:T(8,128)(2,1)S(1)}, u32[]{:S(2)}, u32[]{:S(2)}) collective-permute-start(bf16[1024,1024]{1,0:T(8,128)(2,1)S(1)} %select_convert_fusion), channel_id=1, source_target_pairs={{0,2},{1,3},{2,4},{3,5},{4,6},{5,7},{8,10},{9,11},{10,12},{11,13},... | collective-permute-start | bytes 6291464 | tf_op jit(solution)/shard_map/ppermute | solution.py:78
  19.9 21.4 %collective-permute-start.6 = (bf16[1024,256]{1,0:T(8,128)(2,1)S(1)}, bf16[1024,256]{1,0:T(8,128)(2,1)S(1)}, u32[]{:S(2)}, u32[]{:S(2)}) collective-permute-start(bf16[1024,256]{1,0:T(8,128)(2,1)S(1)} %constant_dynamic-slice_fusion.4), channel_id=1, source_target_pairs={{2,8},{3,9},{4,10},{5,11},{6,12},{7,13},{10,0},{11,1},{12,2},{13,3... | collective-permute-start | bytes 1572872 | tf_op jit(solution)/shard_map/ppermute | solution.py:78
  21.3 15.0 %collective-permute-start.4 = (bf16[1024,512]{1,0:T(8,128)(2,1)S(1)}, bf16[1024,512]{1,0:T(8,128)(2,1)S(1)}, u32[]{:S(2)}, u32[]{:S(2)}) collective-permute-start(bf16[1024,512]{1,0:T(8,128)(2,1)S(1)} %constant_dynamic-slice_fusion.3), channel_id=1, source_target_pairs={{0,8},{1,9},{2,10},{3,11},{4,12},{5,13},{6,14},{7,15},{8,0},{9,1},... | collective-permute-start | bytes 3145736 | tf_op jit(solution)/shard_map/ppermute | solution.py:78
  30.6 22.3 %collective-permute-start.7 = (bf16[1024,256]{1,0:T(8,128)(2,1)S(1)}, bf16[1024,256]{1,0:T(8,128)(2,1)S(1)}, u32[]{:S(2)}, u32[]{:S(2)}) collective-permute-start(bf16[1024,256]{1,0:T(8,128)(2,1)S(1)} %constant_dynamic-slice_fusion.2), channel_id=1, source_target_pairs={{2,0},{3,1},{4,2},{5,3},{6,4},{7,5},{10,8},{11,9},{12,10},{13,11},... | collective-permute-start | bytes 1572872 | tf_op jit(solution)/shard_map/ppermute | solution.py:78
  32.0 31.8 %collective-permute-start.10 = (bf16[1024,256]{1,0:T(8,128)(2,1)S(1)}, bf16[1024,256]{1,0:T(8,128)(2,1)S(1)}, u32[]{:S(2)}, u32[]{:S(2)}) collective-permute-start(bf16[1024,256]{1,0:T(8,128)(2,1)S(1)} %constant_dynamic-slice_fusion.1), channel_id=1, source_target_pairs={{2,8},{3,9},{4,10},{5,11},{6,12},{7,13},{10,0},{11,1},{12,2},{13,3... | collective-permute-start | bytes 1572872 | tf_op jit(solution)/shard_map/ppermute | solution.py:78
  36.4 34.9 %collective-permute-start.8 = (bf16[1024,256]{1,0:T(8,128)(2,1)S(1)}, bf16[1024,256]{1,0:T(8,128)(2,1)S(1)}, u32[]{:S(2)}, u32[]{:S(2)}) collective-permute-start(bf16[1024,256]{1,0:T(8,128)(2,1)S(1)} %broadcast_select_fusion.3), channel_id=1, source_target_pairs={{0,1},{1,0},{2,3},{3,2},{4,5},{5,4},{6,7},{7,6},{8,9},{9,8},{10,11... | collective-permute-start | bytes 1572872 | tf_op jit(solution)/shard_map/ppermute | solution.py:78
  41.4 29.1 %collective-permute-start.9 = (bf16[1024,256]{1,0:T(8,128)(2,1)S(1)}, bf16[1024,256]{1,0:T(8,128)(2,1)S(1)}, u32[]{:S(2)}, u32[]{:S(2)}) collective-permute-start(bf16[1024,256]{1,0:T(8,128)(2,1)S(1)} %broadcast_select_fusion.2), channel_id=1, source_target_pairs={{0,1},{1,8},{2,3},{3,10},{4,5},{5,12},{6,7},{7,14},{8,9},{9,0},{10... | collective-permute-start | bytes 1572872 | tf_op jit(solution)/shard_map/ppermute | solution.py:78
  53.0 44.1 %collective-permute-start.13 = (bf16[1024,256]{1,0:T(8,128)(2,1)S(1)}, bf16[1024,256]{1,0:T(8,128)(2,1)S(1)}, u32[]{:S(2)}, u32[]{:S(2)}) collective-permute-start(bf16[1024,256]{1,0:T(8,128)(2,1)S(1)} %broadcast_select_fusion.1), channel_id=1, source_target_pairs={{0,1},{1,0},{2,3},{3,2},{4,5},{5,4},{6,7},{7,6},{8,9},{9,8},{10,11... | collective-permute-start | bytes 1572872 | tf_op jit(solution)/shard_map/ppermute | solution.py:78
  63.8 27.3 %collective-permute-start.5 = (bf16[1024,512]{1,0:T(8,128)(2,1)S(1)}, bf16[1024,512]{1,0:T(8,128)(2,1)S(1)}, u32[]{:S(2)}, u32[]{:S(2)}) collective-permute-start(bf16[1024,512]{1,0:T(8,128)(2,1)S(1)} %add_convert_fusion), channel_id=1, source_target_pairs={{16,0},{17,1},{18,2},{19,3},{20,4},{21,5},{22,6},{23,7},{24,8},{25... | collective-permute-start | bytes 3145736 | tf_op jit(solution)/shard_map/ppermute | solution.py:78
  65.8 49.9 %collective-permute-start.23 = (bf16[1024,256]{1,0:T(8,128)(2,1)S(1)}, bf16[1024,256]{1,0:T(8,128)(2,1)S(1)}, u32[]{:S(2)}, u32[]{:S(2)}) collective-permute-start(bf16[1024,256]{1,0:T(8,128)(2,1)S(1)} %fusion), channel_id=1, source_target_pairs={{0,16},{1,17},{2,18},{3,19},{4,20},{5,21},{6,22},{7,23},{8,24},{9,... | collective-permute-start | bytes 1572872 | tf_op jit(solution)/shard_map/ppermute | solution.py:78
  70.5 22.3 %collective-permute-start.15 = (bf16[1024,1024]{1,0:T(8,128)(2,1)S(1)}, bf16[1024,1024]{1,0:T(8,128)(2,1)S(1)}, u32[]{:S(2)}, u32[]{:S(2)}) collective-permute-start(bf16[1024,1024]{1,0:T(8,128)(2,1)S(1)} %collective-permute-done.14), channel_id=1, source_target_pairs={{0,8},{1,9},{2,10},{3,11},{4,12},{5,13},{6,14},{7,15},{8,0},{9,1},... | collective-permute-start | bytes 6291464 | tf_op jit(solution)/shard_map/ppermute | solution.py:78
  72.2 25.7 %collective-permute-start.12 = (bf16[1024,256]{1,0:T(8,128)(2,1)S(1)}, bf16[1024,256]{1,0:T(8,128)(2,1)S(1)}, u32[]{:S(2)}, u32[]{:S(2)}) collective-permute-start(bf16[1024,256]{1,0:T(8,128)(2,1)S(1)} %broadcast_select_fusion), channel_id=1, source_target_pairs={{0,1},{1,8},{2,3},{3,10},{4,5},{5,12},{6,7},{7,14},{8,9},{9,0},{10... | collective-permute-start | bytes 1572872 | tf_op jit(solution)/shard_map/ppermute | solution.py:78
  91.0 22.3 %collective-permute-start.24 = (bf16[1536,256]{1,0:T(8,128)(2,1)S(1)}, bf16[1536,256]{1,0:T(8,128)(2,1)S(1)}, u32[]{:S(2)}, u32[]{:S(2)}) collective-permute-start(bf16[1536,256]{1,0:T(8,128)(2,1)S(1)} %pad_maximum_fusion.1), channel_id=1, source_target_pairs={{16,0},{17,1},{18,2},{19,3},{20,4},{21,5},{22,6},{23,7},{24,8},{25... | collective-permute-start | bytes 2359304 | tf_op jit(solution)/shard_map/ppermute | solution.py:78
  94.4 19.6 %collective-permute-start.26 = (bf16[1024,256]{1,0:T(8,128)(2,1)S(1)}, bf16[1024,256]{1,0:T(8,128)(2,1)S(1)}, u32[]{:S(2)}, u32[]{:S(2)}) collective-permute-start(bf16[1024,256]{1,0:T(8,128)(2,1)S(1)} %fusion.3), channel_id=1, source_target_pairs={{2,16},{3,17},{4,18},{5,19},{6,20},{7,21},{10,24},{11,25},{12,26},... | collective-permute-start | bytes 1572872 | tf_op jit(solution)/shard_map/ppermute | solution.py:78
  97.1 17.6 %collective-permute-start.25 = (bf16[1024,256]{1,0:T(8,128)(2,1)S(1)}, bf16[1024,256]{1,0:T(8,128)(2,1)S(1)}, u32[]{:S(2)}, u32[]{:S(2)}) collective-permute-start(bf16[1024,256]{1,0:T(8,128)(2,1)S(1)} %fusion.3), channel_id=1, source_target_pairs={{18,16},{19,17},{20,18},{21,19},{22,20},{23,21},{26,24},{27,25},{2... | collective-permute-start | bytes 1572872 | tf_op jit(solution)/shard_map/ppermute | solution.py:78
  101.0 27.7 %collective-permute-start.16 = (bf16[1536,256]{1,0:T(8,128)(2,1)S(1)}, bf16[1536,256]{1,0:T(8,128)(2,1)S(1)}, u32[]{:S(2)}, u32[]{:S(2)}) collective-permute-start(bf16[1536,256]{1,0:T(8,128)(2,1)S(1)} %pad_maximum_fusion), channel_id=1, source_target_pairs={{16,0},{17,1},{18,2},{19,3},{20,4},{21,5},{22,6},{23,7},{24,8},{25... | collective-permute-start | bytes 2359304 | tf_op jit(solution)/shard_map/ppermute | solution.py:78
  113.3 24.3 %collective-permute-start.19 = (bf16[512,256]{1,0:T(8,128)(2,1)S(1)}, bf16[512,256]{1,0:T(8,128)(2,1)S(1)}, u32[]{:S(2)}, u32[]{:S(2)}) collective-permute-start(bf16[512,256]{1,0:T(8,128)(2,1)S(1)} %get-tuple-element.69), channel_id=1, source_target_pairs={{8,24},{9,25},{10,26},{11,27},{12,28},{13,29},{14,30},{15,31}} | collective-permute-start | bytes 786440 | tf_op jit(solution)/shard_map/ppermute | solution.py:78
  114.0 5.4 %collective-permute-start.18 = (bf16[1024,256]{1,0:T(8,128)(2,1)S(1)}, bf16[1024,256]{1,0:T(8,128)(2,1)S(1)}, u32[]{:S(2)}, u32[]{:S(2)}) collective-permute-start(bf16[1024,256]{1,0:T(8,128)(2,1)S(1)} %fusion.5), channel_id=1, source_target_pairs={{2,16},{3,17},{4,18},{5,19},{6,20},{7,21},{10,24},{11,25},{12,26},... | collective-permute-start | bytes 1572872 | tf_op jit(solution)/shard_map/ppermute | solution.py:78
  115.7 21.9 %collective-permute-start.11 = (bf16[512,256]{1,0:T(8,128)(2,1)S(1)}, bf16[512,256]{1,0:T(8,128)(2,1)S(1)}, u32[]{:S(2)}, u32[]{:S(2)}) collective-permute-start(bf16[512,256]{1,0:T(8,128)(2,1)S(1)} %get-tuple-element.68), channel_id=1, source_target_pairs={{0,16},{1,17},{2,18},{3,19},{4,20},{5,21},{6,22},{7,23},{8,24},{9,... | collective-permute-start | bytes 786440 | tf_op jit(solution)/shard_map/ppermute | solution.py:78
  119.4 19.0 %collective-permute-start.22 = (bf16[1024,256]{1,0:T(8,128)(2,1)S(1)}, bf16[1024,256]{1,0:T(8,128)(2,1)S(1)}, u32[]{:S(2)}, u32[]{:S(2)}) collective-permute-start(bf16[1024,256]{1,0:T(8,128)(2,1)S(1)} %pad_maximum_fusion.3), channel_id=1, source_target_pairs={{2,24},{3,25},{4,26},{5,27},{6,28},{7,29}} | collective-permute-start | bytes 1572872 | tf_op jit(solution)/shard_map/ppermute | solution.py:78
  120.1 18.3 %collective-permute-start.21 = (bf16[1024,256]{1,0:T(8,128)(2,1)S(1)}, bf16[1024,256]{1,0:T(8,128)(2,1)S(1)}, u32[]{:S(2)}, u32[]{:S(2)}) collective-permute-start(bf16[1024,256]{1,0:T(8,128)(2,1)S(1)} %pad_maximum_fusion.3), channel_id=1, source_target_pairs={{18,24},{19,25},{20,26},{21,27},{22,28},{23,29}} | collective-permute-start | bytes 1572872 | tf_op jit(solution)/shard_map/ppermute | solution.py:78
  128.7 9.7 %collective-permute-start.27 = (bf16[1024,256]{1,0:T(8,128)(2,1)S(1)}, bf16[1024,256]{1,0:T(8,128)(2,1)S(1)}, u32[]{:S(2)}, u32[]{:S(2)}) collective-permute-start(bf16[1024,256]{1,0:T(8,128)(2,1)S(1)} %pad_maximum_fusion.4), channel_id=1, source_target_pairs={{0,8},{1,9},{2,10},{3,11},{4,12},{5,13},{6,14},{7,15},{8,0},{9,1},... | collective-permute-start | bytes 1572872 | tf_op jit(solution)/shard_map/ppermute | solution.py:78
  (4 other events, 13.4 us)

commit v3 on v2

--- a/solution.py
+++ b/solution.py
@@ -1,5 +1,3 @@
-import functools
-
 import jax
 import jax.numpy as jnp
 from jax import lax
@@ -17,48 +15,51 @@
     return lax.dot_general(rows, cols, (((0,), (0,)), ((), ())), preferred_element_type=jnp.float32)
 
 
-def merge_body(part, core_ref, keep_top, keep_low, got_top, got_low, *refs):
+def merge_body(core_ref, *refs):
     out_ref, buffer, wide, sems = refs[-4:]
     core = core_ref[0]
 
-    def put(k, source, row, col):
+    def put(k, source, row, col, part):
         start = pl.multiple_of((2 * col + part) * WIDTH, WIDTH)
         return pltpu.make_async_copy(source, out_ref.at[pl.ds(row * TILE, TILE), pl.ds(start, WIDTH)], sems.at[k])
 
-    fetch = pltpu.make_async_copy(got_top, buffer, sems.at[4])
-    fetch.start()
-    copies = [put(0, keep_top, 0, core), put(1, keep_low, 1, 1 - core), put(2, got_low, 1, core)]
-    for copy in copies:
+    fetches, copies = [], []
+    for part in (0, 1):
+        keep_top, keep_low, got_top, got_low = refs[4 * part : 4 * part + 4]
+        fetches.append(pltpu.make_async_copy(got_top, buffer.at[part], sems.at[part]))
+        copies.append(put(2 + part, keep_top, 0, core, part))
+        copies.append(put(4 + part, keep_low, 1, 1 - core, part))
+        copies.append(put(6 + part, got_low, 1, core, part))
+    for copy in fetches + copies:
         copy.start()
-    fetch.wait()
-    wide[...] = buffer[...].astype(jnp.float32)
-    last = put(3, wide, 0, 1 - core)
-    last.start()
+    for part in (0, 1):
+        fetches[part].wait()
+        wide[part] = buffer[part].astype(jnp.float32)
+        last = put(8 + part, wide.at[part], 0, 1 - core, part)
+        last.start()
+        copies.append(last)
     for copy in copies:
         copy.wait()
-    last.wait()
-
-
-def merge(part, core, tiles, into, columns):
+
+
+def merge(core, tiles, columns):
     vmem, anywhere = pl.BlockSpec(memory_space=pltpu.VMEM), pl.BlockSpec(memory_space=pl.ANY)
-    tiles = tiles + (() if into is None else (into,))
     return pl.pallas_call(
-        functools.partial(merge_body, part),
+        merge_body,
         grid_spec=pltpu.PrefetchScalarGridSpec(
             num_scalar_prefetch=1,
             grid=(1,),
-            in_specs=[vmem, vmem, anywhere, vmem] + [anywhere] * (len(tiles) - 4),
+            in_specs=[vmem, vmem, anywhere, vmem] * 2,
             out_specs=anywhere,
             scratch_shapes=[
-                pltpu.VMEM((TILE, WIDTH), jnp.bfloat16),
-                pltpu.VMEM((TILE, WIDTH), jnp.float32),
-                pltpu.SemaphoreType.DMA((5,)),
+                pltpu.VMEM((2, TILE, WIDTH), jnp.bfloat16),
+                pltpu.VMEM((2, TILE, WIDTH), jnp.float32),
+                pltpu.SemaphoreType.DMA((10,)),
             ],
         ),
         out_shape=jax.ShapeDtypeStruct((2 * TILE, columns), jnp.float32),
-        input_output_aliases={} if into is None else {5: 0},
         compiler_params=pltpu.CompilerParams(vmem_limit_bytes=8 * 2**20),
-        cost_estimate=pl.CostEstimate(flops=TILE * columns, bytes_accessed=4 * TILE * columns, transcendentals=0),
+        cost_estimate=pl.CostEstimate(flops=TILE * columns, bytes_accessed=8 * TILE * columns, transcendentals=0),
     )(core, *tiles)
 
 
@@ -116,8 +117,7 @@
         present = (genotypes >= 0).astype(f32)
         dosage = genotypes * present
         stats = jnp.stack([jnp.sum(present, axis=0), jnp.sum(dosage, axis=0), jnp.sum(dosage * dosage, axis=0)])
-        stats = stats + core_swap(stats)
-        stats = stats + x_swap(stats)
+        stats = x_swap(stats) + perm(stats, lambda xx, c, p: (1 - xx, 1 - c, p)) + (stats + core_swap(stats))
         average = stats[1] / stats[0]
         factor = lax.rsqrt(stats[0] * (stats[2] / stats[0] - average * average))
         scale = lax.optimization_barrier(jnp.stack([average, factor]))
@@ -199,7 +199,7 @@
         send_d3(1)
 
         core_arg = core[None].astype(jnp.int32)
-        out = None
+        tiles = []
         for j in (0, 1):
             cols = slice(j * WIDTH, (j + 1) * WIDTH)
             s0 = d0[:, cols].astype(f32) + x_d0[:, cols].astype(f32)
@@ -220,8 +220,8 @@
             send = jnp.concatenate([give_top, early_low.astype(bf16)], axis=0)
             got = core_swap(send)
             got_low = jnp.where(x_first | first_core, got[TILE:].astype(f32), q_sum)
-            out = merge(j, core_arg, (keep_top, late[TILE:], got[:TILE], got_low), out, snps)
-        return out
+            tiles += [keep_top, late[TILE:], got[:TILE], got_low]
+        return merge(core_arg, tiles, snps)
 
     return on_device
 

time: 144 us -> 146 us (1.014)
  waiting for transfers between devices: 75.7 us -> 79.6 us
    ppermute x28 -> x29, waiting for transfers between devices: 75.7 us -> 79.6 us  [perm(): return lax.ppermute(x, axes, pairs)]
    ppermute x28 -> x29, starting transfers between devices: 37.7 us -> 36.5 us  [perm(): return lax.ppermute(x, axes, pairs)]
  transfers between devices with their start and end apart: 28 -> 29, of which waited for: 11 -> 12; matrix products, arithmetic and copies ran while one was open for 13% -> 13% of each run, Pallas kernels for 0% -> 0%
where the time goes in v3:
time: 146 us; the launch traced here: 145 us
  waiting for transfers between devices  79.6 us (55%)
  starting transfers between devices  36.5 us (25%)
  matrix products  13.5 us (9%)
  other arithmetic  11.8 us (8%)
  Pallas kernels  2.13 us (1%)
    ppermute x29, waiting for transfers between devices, perm(): return lax.ppermute(x, axes, pairs)  79.6 us
    ppermute x29, starting transfers between devices, perm(): return lax.ppermute(x, axes, pairs)  36.5 us
    dot_general x18, matrix products, dot_t(): lax.dot_general(rows, cols, (((0,), (0,)), ((), ())), preferred_element_t...  13.5 us
    convert_element_type x2, other arithmetic, standardized(): return jnp.where(g >= 0, (g - by[0]) * by[1], 0.0).astype(bf16)  4.22 us
    reduce_sum x1, other arithmetic, on_device(): jnp.sum(present, axis=0)  3.16 us
  transfers between devices with their start and end apart: 29, of which 12 were waited for; matrix products, arithmetic and copies ran while one was open for 13% of the time, Pallas kernels for 0%

profile of v3, /device:TPU:0, one launch (start us, length us, event | category | flops | bytes accessed | tf_op | source)
XLA Modules:
  0.0 145.1 jit_solution(11741896940739070351)
XLA Ops:
  0.0 3.2 %convert_reduce_fusion = (f32[1024]{0:T(1024)S(1)}, f32[1024]{0:T(1024)S(1)}, f32[1024]{0:T(1024)S(1)}) fusion(f32[1024,1024]{1,0:T(8,128)} %param.1), kind=kLoop, calls=%fused_computation.2 | loop fusion | flops 7336960 | bytes 4206592 | tf_op jit(solution)/shard_map/reduce_sum | solution.py:119
  3.2 3.0 %collective-permute-start = (f32[3,1024]{1,0:T(4,128)S(1)}, f32[3,1024]{1,0:T(4,128)S(1)}, u32[]{:S(2)}, u32[]{:S(2)}) collective-permute-start(f32[3,1024]{1,0:T(4,128)S(1)} %pad_maximum_fusion.5), channel_id=1, source_target_pairs={{0,16},{1,17},{2,18},{3,19},{4,20},{5,21},{6,22},{7,23},{8,24},{9,... | collective-permute-start | bytes 36872 | tf_op jit(solution)/shard_map/ppermute | solution.py:79
  6.4 1.5 %collective-permute-done = f32[3,1024]{1,0:T(4,128)S(1)} collective-permute-done((f32[3,1024]{1,0:T(4,128)S(1)}, f32[3,1024]{1,0:T(4,128)S(1)}, u32[]{:S(2)}, u32[]{:S(2)}) %collective-permute-start) | collective-permute-done | bytes 12320 | tf_op jit(solution)/shard_map/ppermute | solution.py:79
  11.0 2.8 %select_convert_fusion = bf16[1024,1024]{1,0:T(8,128)(2,1)S(1)} fusion(f32[1024,1024]{1,0:T(8,128)} %param.1, f32[1024]{0:T(1024)S(1)} %bitcast.48, f32[1024]{0:T(1024)S(1)} %bitcast.47), kind=kLoop, calls=%fused_computation | loop fusion | flops 5242880 | bytes 6299648 | tf_op jit(solution)/shard_map/convert_element_type | solution.py:129
  16.6 5.3 %collective-permute-start.13 = (bf16[1024,1024]{1,0:T(8,128)(2,1)S(1)}, bf16[1024,1024]{1,0:T(8,128)(2,1)S(1)}, u32[]{:S(2)}, u32[]{:S(2)}) collective-permute-start(bf16[1024,1024]{1,0:T(8,128)(2,1)S(1)} %select_convert_fusion), channel_id=1, source_target_pairs={{0,2},{1,3},{2,4},{3,5},{4,6},{5,7},{8,10},{9,11},{10,12},{11,13},... | collective-permute-start | bytes 6291464 | tf_op jit(solution)/shard_map/ppermute | solution.py:79
  22.1 8.4 %collective-permute-done.4 = bf16[1024,256]{1,0:T(8,128)(2,1)S(1)} collective-permute-done((bf16[1024,256]{1,0:T(8,128)(2,1)S(1)}, bf16[1024,256]{1,0:T(8,128)(2,1)S(1)}, u32[]{:S(2)}, u32[]{:S(2)}) %collective-permute-start.4) | collective-permute-done | bytes 524320 | tf_op jit(solution)/shard_map/ppermute | solution.py:79
  32.1 1.6 %collective-permute-start.10 = (bf16[1024,256]{1,0:T(8,128)(2,1)S(1)}, bf16[1024,256]{1,0:T(8,128)(2,1)S(1)}, u32[]{:S(2)}, u32[]{:S(2)}) collective-permute-start(bf16[1024,256]{1,0:T(8,128)(2,1)S(1)} %broadcast_select_fusion.3), channel_id=1, source_target_pairs={{0,1},{1,0},{2,3},{3,2},{4,5},{5,4},{6,7},{7,6},{8,9},{9,8},{10,11... | collective-permute-start | bytes 1572872 | tf_op jit(solution)/shard_map/ppermute | solution.py:79
  33.7 1.8 %broadcast_maximum_fusion.2 = bf16[1024,1024]{1,0:T(8,128)(2,1)S(1)} fusion(bf16[1024,1024]{1,0:T(8,128)(2,1)} %collective-permute-done.3), kind=kLoop, calls=%fused_computation.29 | loop fusion | flops 1048576 | bytes 4194304 | tf_op jit(solution)/shard_map/max | solution.py:132
  39.3 1.5 %collective-permute-done.7 = bf16[1024,256]{1,0:T(8,128)(2,1)S(1)} collective-permute-done((bf16[1024,256]{1,0:T(8,128)(2,1)S(1)}, bf16[1024,256]{1,0:T(8,128)(2,1)S(1)}, u32[]{:S(2)}, u32[]{:S(2)}) %collective-permute-start.7) | collective-permute-done | bytes 524320 | tf_op jit(solution)/shard_map/ppermute | solution.py:79
  40.9 1.6 %collective-permute-start.11 = (bf16[1024,256]{1,0:T(8,128)(2,1)S(1)}, bf16[1024,256]{1,0:T(8,128)(2,1)S(1)}, u32[]{:S(2)}, u32[]{:S(2)}) collective-permute-start(bf16[1024,256]{1,0:T(8,128)(2,1)S(1)} %broadcast_select_fusion.2), channel_id=1, source_target_pairs={{0,1},{1,8},{2,3},{3,10},{4,5},{5,12},{6,7},{7,14},{8,9},{9,0},{10... | collective-permute-start | bytes 1572872 | tf_op jit(solution)/shard_map/ppermute | solution.py:79
  44.0 9.1 %collective-permute-done.9 = bf16[1024,256]{1,0:T(8,128)(2,1)S(1)} collective-permute-done((bf16[1024,256]{1,0:T(8,128)(2,1)S(1)}, bf16[1024,256]{1,0:T(8,128)(2,1)S(1)}, u32[]{:S(2)}, u32[]{:S(2)}) %collective-permute-start.9) | collective-permute-done | bytes 524320 | tf_op jit(solution)/shard_map/ppermute | solution.py:79
  53.1 1.6 %collective-permute-start.23 = (bf16[1024,256]{1,0:T(8,128)(2,1)S(1)}, bf16[1024,256]{1,0:T(8,128)(2,1)S(1)}, u32[]{:S(2)}, u32[]{:S(2)}) collective-permute-start(bf16[1024,256]{1,0:T(8,128)(2,1)S(1)} %broadcast_select_fusion.1), channel_id=1, source_target_pairs={{0,1},{1,0},{2,3},{3,2},{4,5},{5,4},{6,7},{7,6},{8,9},{9,8},{10,11... | collective-permute-start | bytes 1572872 | tf_op jit(solution)/shard_map/ppermute | solution.py:79
  54.7 8.6 %collective-permute-done.14 = bf16[1024,256]{1,0:T(8,128)(2,1)S(1)} collective-permute-done((bf16[1024,256]{1,0:T(8,128)(2,1)S(1)}, bf16[1024,256]{1,0:T(8,128)(2,1)S(1)}, u32[]{:S(2)}, u32[]{:S(2)}) %collective-permute-start.14) | collective-permute-done | bytes 524320 | tf_op jit(solution)/shard_map/ppermute | solution.py:79
  65.3 1.7 %collective-permute-done.13 = bf16[1024,1024]{1,0:T(8,128)(2,1)S(1)} collective-permute-done((bf16[1024,1024]{1,0:T(8,128)(2,1)S(1)}, bf16[1024,1024]{1,0:T(8,128)(2,1)S(1)}, u32[]{:S(2)}, u32[]{:S(2)}) %collective-permute-start.13) | collective-permute-done | bytes 2097184 | tf_op jit(solution)/shard_map/ppermute | solution.py:79
  67.0 2.9 %collective-permute-start.8 = (bf16[1024,256]{1,0:T(8,128)(2,1)S(1)}, bf16[1024,256]{1,0:T(8,128)(2,1)S(1)}, u32[]{:S(2)}, u32[]{:S(2)}) collective-permute-start(bf16[1024,256]{1,0:T(8,128)(2,1)S(1)} %fusion), channel_id=1, source_target_pairs={{0,16},{1,17},{2,18},{3,19},{4,20},{5,21},{6,22},{7,23},{8,24},{9,... | collective-permute-start | bytes 1572872 | tf_op jit(solution)/shard_map/ppermute | solution.py:79
  71.7 1.6 %collective-permute-start.22 = (bf16[1024,256]{1,0:T(8,128)(2,1)S(1)}, bf16[1024,256]{1,0:T(8,128)(2,1)S(1)}, u32[]{:S(2)}, u32[]{:S(2)}) collective-permute-start(bf16[1024,256]{1,0:T(8,128)(2,1)S(1)} %broadcast_select_fusion), channel_id=1, source_target_pairs={{0,1},{1,8},{2,3},{3,10},{4,5},{5,12},{6,7},{7,14},{8,9},{9,0},{10... | collective-permute-start | bytes 1572872 | tf_op jit(solution)/shard_map/ppermute | solution.py:79
  74.5 16.4 %collective-permute-done.6 = bf16[1024,512]{1,0:T(8,128)(2,1)S(1)} collective-permute-done((bf16[1024,512]{1,0:T(8,128)(2,1)S(1)}, bf16[1024,512]{1,0:T(8,128)(2,1)S(1)}, u32[]{:S(2)}, u32[]{:S(2)}) %collective-permute-start.6) | collective-permute-done | bytes 1048608 | tf_op jit(solution)/shard_map/ppermute | solution.py:79
  90.9 1.5 %collective-permute-start.12 = (bf16[1536,256]{1,0:T(8,128)(2,1)S(1)}, bf16[1536,256]{1,0:T(8,128)(2,1)S(1)}, u32[]{:S(2)}, u32[]{:S(2)}) collective-permute-start(bf16[1536,256]{1,0:T(8,128)(2,1)S(1)} %pad_maximum_fusion), channel_id=1, source_target_pairs={{16,0},{17,1},{18,2},{19,3},{20,4},{21,5},{22,6},{23,7},{24,8},{25... | collective-permute-start | bytes 2359304 | tf_op jit(solution)/shard_map/ppermute | solution.py:79
  102.2 11.0 %collective-permute-done.12 = bf16[1536,256]{1,0:T(8,128)(2,1)S(1)} collective-permute-done((bf16[1536,256]{1,0:T(8,128)(2,1)S(1)}, bf16[1536,256]{1,0:T(8,128)(2,1)S(1)}, u32[]{:S(2)}, u32[]{:S(2)}) %collective-permute-start.12) | collective-permute-done | bytes 786464 | tf_op jit(solution)/shard_map/ppermute | solution.py:79
  115.5 4.3 %collective-permute-start.21 = (bf16[512,256]{1,0:T(8,128)(2,1)S(1)}, bf16[512,256]{1,0:T(8,128)(2,1)S(1)}, u32[]{:S(2)}, u32[]{:S(2)}) collective-permute-start(bf16[512,256]{1,0:T(8,128)(2,1)S(1)} %get-tuple-element.68), channel_id=1, source_target_pairs={{0,16},{1,17},{2,18},{3,19},{4,20},{5,21},{6,22},{7,23},{8,24},{9,... | collective-permute-start | bytes 786440 | tf_op jit(solution)/shard_map/ppermute | solution.py:79
  121.6 7.2 %collective-permute-done.24 = bf16[1536,256]{1,0:T(8,128)(2,1)S(1)} collective-permute-done((bf16[1536,256]{1,0:T(8,128)(2,1)S(1)}, bf16[1536,256]{1,0:T(8,128)(2,1)S(1)}, u32[]{:S(2)}, u32[]{:S(2)}) %collective-permute-start.24) | collective-permute-done | bytes 786464 | tf_op jit(solution)/shard_map/ppermute | solution.py:79
  129.0 11.2 %collective-permute-done.21 = bf16[512,256]{1,0:T(8,128)(2,1)S(1)} collective-permute-done((bf16[512,256]{1,0:T(8,128)(2,1)S(1)}, bf16[512,256]{1,0:T(8,128)(2,1)S(1)}, u32[]{:S(2)}, u32[]{:S(2)}) %collective-permute-start.21) | collective-permute-done | bytes 262176 | tf_op jit(solution)/shard_map/ppermute | solution.py:79
  141.0 1.6 %collective-permute-done.28 = bf16[1024,256]{1,0:T(8,128)(2,1)S(1)} collective-permute-done((bf16[1024,256]{1,0:T(8,128)(2,1)S(1)}, bf16[1024,256]{1,0:T(8,128)(2,1)S(1)}, u32[]{:S(2)}, u32[]{:S(2)}) %collective-permute-start.28) | collective-permute-done | bytes 524320 | tf_op jit(solution)/shard_map/ppermute | solution.py:79
  142.8 2.1 %shard_map.17 = f32[1024,1024]{1,0:T(8,128)} custom-call(s32[1]{0:T(128)} %bitcast.core_ref, f32[512,256]{1,0:T(8,128)S(1)} %get-tuple-element.67.refs_0_, f32[512,256]{1,0:T(8,128)S(1)} %get-tuple-element.66.refs_1_, bf16[512,256]{1,0:T(8,128)(2,1)S(1)} %slice.179.refs_2_, f32[512,256]{1,0:T(8,128)S(1)} %get-tuple-element.63.refs_3_, ...), custom_call_target="tpu_custom_call" | custom-call | flops 524288 | bytes 4194304 | tf_op jit(solution)/shard_map/pallas_call | solution.py:47
  (93 shorter events, 32.8 us)
Async XLA Ops:
  13.8 18.3 %collective-permute-start.3 = (bf16[1024,1024]{1,0:T(8,128)(2,1)S(1)}, bf16[1024,1024]{1,0:T(8,128)(2,1)}, u32[]{:S(2)}, u32[]{:S(2)}) collective-permute-start(bf16[1024,1024]{1,0:T(8,128)(2,1)S(1)} %select_convert_fusion), channel_id=1, source_target_pairs={{0,8},{1,9},{2,10},{3,11},{4,12},{5,13},{6,14},{7,15},{8,0},{9,1},... | collective-permute-start | bytes 6291464 | tf_op jit(solution)/shard_map/ppermute | solution.py:79
  13.9 16.7 %collective-permute-start.4 = (bf16[1024,256]{1,0:T(8,128)(2,1)S(1)}, bf16[1024,256]{1,0:T(8,128)(2,1)S(1)}, u32[]{:S(2)}, u32[]{:S(2)}) collective-permute-start(bf16[1024,256]{1,0:T(8,128)(2,1)S(1)} %select_convert_fusion.1), channel_id=1, source_target_pairs={{2,0},{3,1},{4,2},{5,3},{6,4},{7,5},{10,8},{11,9},{12,10},{13,11},... | collective-permute-start | bytes 1572872 | tf_op jit(solution)/shard_map/ppermute | solution.py:79
  15.3 25.5 %collective-permute-start.7 = (bf16[1024,256]{1,0:T(8,128)(2,1)S(1)}, bf16[1024,256]{1,0:T(8,128)(2,1)S(1)}, u32[]{:S(2)}, u32[]{:S(2)}) collective-permute-start(bf16[1024,256]{1,0:T(8,128)(2,1)S(1)} %constant_dynamic-slice_fusion.4), channel_id=1, source_target_pairs={{2,8},{3,9},{4,10},{5,11},{6,12},{7,13},{10,0},{11,1},{12,2},{13,3... | collective-permute-start | bytes 1572872 | tf_op jit(solution)/shard_map/ppermute | solution.py:79
  16.6 50.4 %collective-permute-start.13 = (bf16[1024,1024]{1,0:T(8,128)(2,1)S(1)}, bf16[1024,1024]{1,0:T(8,128)(2,1)S(1)}, u32[]{:S(2)}, u32[]{:S(2)}) collective-permute-start(bf16[1024,1024]{1,0:T(8,128)(2,1)S(1)} %select_convert_fusion), channel_id=1, source_target_pairs={{0,2},{1,3},{2,4},{3,5},{4,6},{5,7},{8,10},{9,11},{10,12},{11,13},... | collective-permute-start | bytes 6291464 | tf_op jit(solution)/shard_map/ppermute | solution.py:79
  22.1 14.7 %collective-permute-start.5 = (bf16[1024,512]{1,0:T(8,128)(2,1)S(1)}, bf16[1024,512]{1,0:T(8,128)(2,1)S(1)}, u32[]{:S(2)}, u32[]{:S(2)}) collective-permute-start(bf16[1024,512]{1,0:T(8,128)(2,1)S(1)} %constant_dynamic-slice_fusion.3), channel_id=1, source_target_pairs={{0,8},{1,9},{2,10},{3,11},{4,12},{5,13},{6,14},{7,15},{8,0},{9,1},... | collective-permute-start | bytes 3145736 | tf_op jit(solution)/shard_map/ppermute | solution.py:79
  30.7 22.3 %collective-permute-start.9 = (bf16[1024,256]{1,0:T(8,128)(2,1)S(1)}, bf16[1024,256]{1,0:T(8,128)(2,1)S(1)}, u32[]{:S(2)}, u32[]{:S(2)}) collective-permute-start(bf16[1024,256]{1,0:T(8,128)(2,1)S(1)} %constant_dynamic-slice_fusion.2), channel_id=1, source_target_pairs={{2,0},{3,1},{4,2},{5,3},{6,4},{7,5},{10,8},{11,9},{12,10},{13,11},... | collective-permute-start | bytes 1572872 | tf_op jit(solution)/shard_map/ppermute | solution.py:79
  32.1 38.8 %collective-permute-start.10 = (bf16[1024,256]{1,0:T(8,128)(2,1)S(1)}, bf16[1024,256]{1,0:T(8,128)(2,1)S(1)}, u32[]{:S(2)}, u32[]{:S(2)}) collective-permute-start(bf16[1024,256]{1,0:T(8,128)(2,1)S(1)} %broadcast_select_fusion.3), channel_id=1, source_target_pairs={{0,1},{1,0},{2,3},{3,2},{4,5},{5,4},{6,7},{7,6},{8,9},{9,8},{10,11... | collective-permute-start | bytes 1572872 | tf_op jit(solution)/shard_map/ppermute | solution.py:79
  36.8 26.5 %collective-permute-start.14 = (bf16[1024,256]{1,0:T(8,128)(2,1)S(1)}, bf16[1024,256]{1,0:T(8,128)(2,1)S(1)}, u32[]{:S(2)}, u32[]{:S(2)}) collective-permute-start(bf16[1024,256]{1,0:T(8,128)(2,1)S(1)} %constant_dynamic-slice_fusion.1), channel_id=1, source_target_pairs={{2,8},{3,9},{4,10},{5,11},{6,12},{7,13},{10,0},{11,1},{12,2},{13,3... | collective-permute-start | bytes 1572872 | tf_op jit(solution)/shard_map/ppermute | solution.py:79
  40.9 29.1 %collective-permute-start.11 = (bf16[1024,256]{1,0:T(8,128)(2,1)S(1)}, bf16[1024,256]{1,0:T(8,128)(2,1)S(1)}, u32[]{:S(2)}, u32[]{:S(2)}) collective-permute-start(bf16[1024,256]{1,0:T(8,128)(2,1)S(1)} %broadcast_select_fusion.2), channel_id=1, source_target_pairs={{0,1},{1,8},{2,3},{3,10},{4,5},{5,12},{6,7},{7,14},{8,9},{9,0},{10... | collective-permute-start | bytes 1572872 | tf_op jit(solution)/shard_map/ppermute | solution.py:79
  53.1 43.8 %collective-permute-start.23 = (bf16[1024,256]{1,0:T(8,128)(2,1)S(1)}, bf16[1024,256]{1,0:T(8,128)(2,1)S(1)}, u32[]{:S(2)}, u32[]{:S(2)}) collective-permute-start(bf16[1024,256]{1,0:T(8,128)(2,1)S(1)} %broadcast_select_fusion.1), channel_id=1, source_target_pairs={{0,1},{1,0},{2,3},{3,2},{4,5},{5,4},{6,7},{7,6},{8,9},{9,8},{10,11... | collective-permute-start | bytes 1572872 | tf_op jit(solution)/shard_map/ppermute | solution.py:79
  63.3 27.5 %collective-permute-start.6 = (bf16[1024,512]{1,0:T(8,128)(2,1)S(1)}, bf16[1024,512]{1,0:T(8,128)(2,1)S(1)}, u32[]{:S(2)}, u32[]{:S(2)}) collective-permute-start(bf16[1024,512]{1,0:T(8,128)(2,1)S(1)} %add_convert_fusion), channel_id=1, source_target_pairs={{16,0},{17,1},{18,2},{19,3},{20,4},{21,5},{22,6},{23,7},{24,8},{25... | collective-permute-start | bytes 3145736 | tf_op jit(solution)/shard_map/ppermute | solution.py:79
  67.0 48.5 %collective-permute-start.8 = (bf16[1024,256]{1,0:T(8,128)(2,1)S(1)}, bf16[1024,256]{1,0:T(8,128)(2,1)S(1)}, u32[]{:S(2)}, u32[]{:S(2)}) collective-permute-start(bf16[1024,256]{1,0:T(8,128)(2,1)S(1)} %fusion), channel_id=1, source_target_pairs={{0,16},{1,17},{2,18},{3,19},{4,20},{5,21},{6,22},{7,23},{8,24},{9,... | collective-permute-start | bytes 1572872 | tf_op jit(solution)/shard_map/ppermute | solution.py:79
  70.0 22.5 %collective-permute-start.15 = (bf16[1024,1024]{1,0:T(8,128)(2,1)S(1)}, bf16[1024,1024]{1,0:T(8,128)(2,1)S(1)}, u32[]{:S(2)}, u32[]{:S(2)}) collective-permute-start(bf16[1024,1024]{1,0:T(8,128)(2,1)S(1)} %collective-permute-done.13), channel_id=1, source_target_pairs={{0,8},{1,9},{2,10},{3,11},{4,12},{5,13},{6,14},{7,15},{8,0},{9,1},... | collective-permute-start | bytes 6291464 | tf_op jit(solution)/shard_map/ppermute | solution.py:79
  71.7 25.9 %collective-permute-start.22 = (bf16[1024,256]{1,0:T(8,128)(2,1)S(1)}, bf16[1024,256]{1,0:T(8,128)(2,1)S(1)}, u32[]{:S(2)}, u32[]{:S(2)}) collective-permute-start(bf16[1024,256]{1,0:T(8,128)(2,1)S(1)} %broadcast_select_fusion), channel_id=1, source_target_pairs={{0,1},{1,8},{2,3},{3,10},{4,5},{5,12},{6,7},{7,14},{8,9},{9,0},{10... | collective-permute-start | bytes 1572872 | tf_op jit(solution)/shard_map/ppermute | solution.py:79
  90.9 22.3 %collective-permute-start.12 = (bf16[1536,256]{1,0:T(8,128)(2,1)S(1)}, bf16[1536,256]{1,0:T(8,128)(2,1)S(1)}, u32[]{:S(2)}, u32[]{:S(2)}) collective-permute-start(bf16[1536,256]{1,0:T(8,128)(2,1)S(1)} %pad_maximum_fusion), channel_id=1, source_target_pairs={{16,0},{17,1},{18,2},{19,3},{20,4},{21,5},{22,6},{23,7},{24,8},{25... | collective-permute-start | bytes 2359304 | tf_op jit(solution)/shard_map/ppermute | solution.py:79
  94.3 19.6 %collective-permute-start.16 = (bf16[1024,256]{1,0:T(8,128)(2,1)S(1)}, bf16[1024,256]{1,0:T(8,128)(2,1)S(1)}, u32[]{:S(2)}, u32[]{:S(2)}) collective-permute-start(bf16[1024,256]{1,0:T(8,128)(2,1)S(1)} %fusion.3), channel_id=1, source_target_pairs={{18,16},{19,17},{20,18},{21,19},{22,20},{23,21},{26,24},{27,25},{2... | collective-permute-start | bytes 1572872 | tf_op jit(solution)/shard_map/ppermute | solution.py:79
  96.9 17.6 %collective-permute-start.17 = (bf16[1024,256]{1,0:T(8,128)(2,1)S(1)}, bf16[1024,256]{1,0:T(8,128)(2,1)S(1)}, u32[]{:S(2)}, u32[]{:S(2)}) collective-permute-start(bf16[1024,256]{1,0:T(8,128)(2,1)S(1)} %fusion.3), channel_id=1, source_target_pairs={{2,16},{3,17},{4,18},{5,19},{6,20},{7,21},{10,24},{11,25},{12,26},... | collective-permute-start | bytes 1572872 | tf_op jit(solution)/shard_map/ppermute | solution.py:79
  99.3 29.5 %collective-permute-start.24 = (bf16[1536,256]{1,0:T(8,128)(2,1)S(1)}, bf16[1536,256]{1,0:T(8,128)(2,1)S(1)}, u32[]{:S(2)}, u32[]{:S(2)}) collective-permute-start(bf16[1536,256]{1,0:T(8,128)(2,1)S(1)} %pad_maximum_fusion.1), channel_id=1, source_target_pairs={{16,0},{17,1},{18,2},{19,3},{20,4},{21,5},{22,6},{23,7},{24,8},{25... | collective-permute-start | bytes 2359304 | tf_op jit(solution)/shard_map/ppermute | solution.py:79
  113.1 27.1 %collective-permute-start.27 = (bf16[512,256]{1,0:T(8,128)(2,1)S(1)}, bf16[512,256]{1,0:T(8,128)(2,1)S(1)}, u32[]{:S(2)}, u32[]{:S(2)}) collective-permute-start(bf16[512,256]{1,0:T(8,128)(2,1)S(1)} %get-tuple-element.69), channel_id=1, source_target_pairs={{8,24},{9,25},{10,26},{11,27},{12,28},{13,29},{14,30},{15,31}} | collective-permute-start | bytes 786440 | tf_op jit(solution)/shard_map/ppermute | solution.py:79
  113.8 6.3 %collective-permute-start.25 = (bf16[1024,256]{1,0:T(8,128)(2,1)S(1)}, bf16[1024,256]{1,0:T(8,128)(2,1)S(1)}, u32[]{:S(2)}, u32[]{:S(2)}) collective-permute-start(bf16[1024,256]{1,0:T(8,128)(2,1)S(1)} %fusion.5), channel_id=1, source_target_pairs={{18,16},{19,17},{20,18},{21,19},{22,20},{23,21},{26,24},{27,25},{2... | collective-permute-start | bytes 1572872 | tf_op jit(solution)/shard_map/ppermute | solution.py:79
  115.5 24.8 %collective-permute-start.21 = (bf16[512,256]{1,0:T(8,128)(2,1)S(1)}, bf16[512,256]{1,0:T(8,128)(2,1)S(1)}, u32[]{:S(2)}, u32[]{:S(2)}) collective-permute-start(bf16[512,256]{1,0:T(8,128)(2,1)S(1)} %get-tuple-element.68), channel_id=1, source_target_pairs={{0,16},{1,17},{2,18},{3,19},{4,20},{5,21},{6,22},{7,23},{8,24},{9,... | collective-permute-start | bytes 786440 | tf_op jit(solution)/shard_map/ppermute | solution.py:79
  120.2 22.4 %collective-permute-start.19 = (bf16[1024,256]{1,0:T(8,128)(2,1)S(1)}, bf16[1024,256]{1,0:T(8,128)(2,1)S(1)}, u32[]{:S(2)}, u32[]{:S(2)}) collective-permute-start(bf16[1024,256]{1,0:T(8,128)(2,1)S(1)} %pad_maximum_fusion.3), channel_id=1, source_target_pairs={{18,24},{19,25},{20,26},{21,27},{22,28},{23,29}} | collective-permute-start | bytes 1572872 | tf_op jit(solution)/shard_map/ppermute | solution.py:79
  120.9 21.7 %collective-permute-start.20 = (bf16[1024,256]{1,0:T(8,128)(2,1)S(1)}, bf16[1024,256]{1,0:T(8,128)(2,1)S(1)}, u32[]{:S(2)}, u32[]{:S(2)}) collective-permute-start(bf16[1024,256]{1,0:T(8,128)(2,1)S(1)} %pad_maximum_fusion.3), channel_id=1, source_target_pairs={{2,24},{3,25},{4,26},{5,27},{6,28},{7,29}} | collective-permute-start | bytes 1572872 | tf_op jit(solution)/shard_map/ppermute | solution.py:79
  128.8 12.2 %collective-permute-start.18 = (bf16[1024,256]{1,0:T(8,128)(2,1)S(1)}, bf16[1024,256]{1,0:T(8,128)(2,1)S(1)}, u32[]{:S(2)}, u32[]{:S(2)}) collective-permute-start(bf16[1024,256]{1,0:T(8,128)(2,1)S(1)} %pad_maximum_fusion.2), channel_id=1, source_target_pairs={{0,8},{1,9},{2,10},{3,11},{4,12},{5,13},{6,14},{7,15},{8,0},{9,1},... | collective-permute-start | bytes 1572872 | tf_op jit(solution)/shard_map/ppermute | solution.py:79
  (5 other events, 19.4 us)

commit v4 on v2

--- a/solution.py
+++ b/solution.py
@@ -177,6 +177,7 @@
         nexts[1].append(relay_cross(1))
         d2.append(pair(rows, above[1]))
         x_top = to_x1(d2[1][:TILE])
+        x_back = perm(d2[1][TILE:], lambda xx, c, p: (0, 0, p) if (xx, c) == (1, 0) else None)
         x_low = perm(d2[1][TILE:], lambda xx, c, p: (1, 1, p) if (xx, c) == (0, 1) else None)
         other_up = core_swap(up)
         below = (step(staged, up), step(staged, other_up))
@@ -194,7 +195,7 @@
         q_far = perm(d4, lambda xx, c, p: (1, 1, p - 2) if (xx, c) == (0, 0) else None)
         nexts[1] = [step(staged, n) for n in nexts[1]]
         d1.append(pair(rows, nexts[1]))
-        part = jnp.concatenate([d1[1], d2[1][TILE:]], axis=0)
+        part = d1[1]
         x_d1.append(to_x0(part))
         send_d3(1)
 
@@ -205,7 +206,7 @@
             s0 = d0[:, cols].astype(f32) + x_d0[:, cols].astype(f32)
             upper, lower = (x_d2[:TILE], x_d2[TILE:]) if j == 0 else (x_top, x_low)
             s2_top = d2[j][:TILE].astype(f32) + upper.astype(f32)
-            s2_low = d2[j][TILE:].astype(f32) + jnp.where(x_first, x_d1[j][snps:], lower).astype(f32)
+            s2_low = d2[j][TILE:].astype(f32) + jnp.where(x_first, x_d1[0][snps:] if j == 0 else x_back, lower).astype(f32)
             early_top = jnp.where(x_first, s0[:TILE], s2_top)
             early_low = jnp.where(first_core | ~x_first, s2_low, s0[TILE:])
             late = jnp.where(

time: 144 us -> 147 us (1.021)
  the two profiles are of different devices: /device:TPU:0 before, /device:TPU:19 now
where the time goes in v4:
time: 147 us
  waiting for transfers between devices  60.6 us (41%)
  starting transfers between devices  56.5 us (38%)
  matrix products  13.5 us (9%)
  other arithmetic  11.8 us (8%)
  Pallas kernels  2.75 us (2%)
    ppermute x29, waiting for transfers between devices, perm(): return lax.ppermute(x, axes, pairs)  60.6 us
    ppermute x29, starting transfers between devices, perm(): return lax.ppermute(x, axes, pairs)  56.5 us
    dot_general x18, matrix products, dot_t(): lax.dot_general(rows, cols, (((0,), (0,)), ((), ())), preferred_element_t...  13.5 us
    convert_element_type x2, other arithmetic, standardized(): return jnp.where(g >= 0, (g - by[0]) * by[1], 0.0).astype(bf16)  4.22 us
    reduce_sum x1, other arithmetic, on_device(): jnp.sum(present, axis=0)  3.16 us
  transfers between devices with their start and end apart: 29, of which 10 were waited for; matrix products, arithmetic and copies ran while one was open for 12% of the time, Pallas kernels for 0%

profile of v4, /device:TPU:19, one launch (start us, length us, event | category | flops | bytes accessed | tf_op | source)
XLA Modules:
  0.0 146.7 jit_solution(326750561544173435)
XLA Ops:
  0.0 3.2 %convert_reduce_fusion = (f32[1024]{0:T(1024)S(1)}, f32[1024]{0:T(1024)S(1)}, f32[1024]{0:T(1024)S(1)}) fusion(f32[1024,1024]{1,0:T(8,128)} %param.1), kind=kLoop, calls=%fused_computation.2 | loop fusion | flops 7336960 | bytes 4206592 | tf_op jit(solution)/shard_map/reduce_sum | solution.py:118
  5.1 2.3 %collective-permute-done.1 = f32[3,1024]{1,0:T(4,128)S(1)} collective-permute-done((f32[3,1024]{1,0:T(4,128)S(1)}, f32[3,1024]{1,0:T(4,128)S(1)}, u32[]{:S(2)}, u32[]{:S(2)}) %collective-permute-start.1) | collective-permute-done | bytes 12320 | tf_op jit(solution)/shard_map/ppermute | solution.py:78
  7.6 1.4 select_convert_fusion.1
  9.0 2.8 %select_convert_fusion = bf16[1024,1024]{1,0:T(8,128)(2,1)S(1)} fusion(f32[1024,1024]{1,0:T(8,128)} %param.1, f32[1024]{0:T(1024)S(1)} %bitcast.51, f32[1024]{0:T(1024)S(1)} %bitcast.50), kind=kLoop, calls=%fused_computation | loop fusion | flops 5242880 | bytes 6299648 | tf_op jit(solution)/shard_map/convert_element_type | solution.py:129
  11.9 1.6 %collective-permute-start.2 = (bf16[1024,1024]{1,0:T(8,128)(2,1)S(1)}, bf16[1024,1024]{1,0:T(8,128)(2,1)}, u32[]{:S(2)}, u32[]{:S(2)}) collective-permute-start(bf16[1024,1024]{1,0:T(8,128)(2,1)S(1)} %select_convert_fusion), channel_id=1, source_target_pairs={{0,8},{1,9},{2,10},{3,11},{4,12},{5,13},{6,14},{7,15},{8,0},{9,1},... | collective-permute-start | bytes 6291464 | tf_op jit(solution)/shard_map/ppermute | solution.py:78
  13.4 2.1 %collective-permute-start.3 = (bf16[1024,256]{1,0:T(8,128)(2,1)S(1)}, bf16[1024,256]{1,0:T(8,128)(2,1)S(1)}, u32[]{:S(2)}, u32[]{:S(2)}) collective-permute-start(bf16[1024,256]{1,0:T(8,128)(2,1)S(1)} %select_convert_fusion.1), channel_id=1, source_target_pairs={{2,0},{3,1},{4,2},{5,3},{6,4},{7,5},{10,8},{11,9},{12,10},{13,11},... | collective-permute-start | bytes 1572872 | tf_op jit(solution)/shard_map/ppermute | solution.py:78
  15.5 3.2 %collective-permute-start.14 = (bf16[1024,1024]{1,0:T(8,128)(2,1)S(1)}, bf16[1024,1024]{1,0:T(8,128)(2,1)S(1)}, u32[]{:S(2)}, u32[]{:S(2)}) collective-permute-start(bf16[1024,1024]{1,0:T(8,128)(2,1)S(1)} %select_convert_fusion), channel_id=1, source_target_pairs={{0,2},{1,3},{2,4},{3,5},{4,6},{5,7},{8,10},{9,11},{10,12},{11,13},... | collective-permute-start | bytes 6291464 | tf_op jit(solution)/shard_map/ppermute | solution.py:78
  18.9 2.5 %collective-permute-start.6 = (bf16[1024,256]{1,0:T(8,128)(2,1)S(1)}, bf16[1024,256]{1,0:T(8,128)(2,1)S(1)}, u32[]{:S(2)}, u32[]{:S(2)}) collective-permute-start(bf16[1024,256]{1,0:T(8,128)(2,1)S(1)} %constant_dynamic-slice_fusion.4), channel_id=1, source_target_pairs={{2,8},{3,9},{4,10},{5,11},{6,12},{7,13},{10,0},{11,1},{12,2},{13,3... | collective-permute-start | bytes 1572872 | tf_op jit(solution)/shard_map/ppermute | solution.py:78
  21.6 7.1 %collective-permute-done.3 = bf16[1024,256]{1,0:T(8,128)(2,1)S(1)} collective-permute-done((bf16[1024,256]{1,0:T(8,128)(2,1)S(1)}, bf16[1024,256]{1,0:T(8,128)(2,1)S(1)}, u32[]{:S(2)}, u32[]{:S(2)}) %collective-permute-start.3) | collective-permute-done | bytes 524320 | tf_op jit(solution)/shard_map/ppermute | solution.py:78
  28.9 2.1 %collective-permute-start.7 = (bf16[1024,256]{1,0:T(8,128)(2,1)S(1)}, bf16[1024,256]{1,0:T(8,128)(2,1)S(1)}, u32[]{:S(2)}, u32[]{:S(2)}) collective-permute-start(bf16[1024,256]{1,0:T(8,128)(2,1)S(1)} %constant_dynamic-slice_fusion.2), channel_id=1, source_target_pairs={{2,0},{3,1},{4,2},{5,3},{6,4},{7,5},{10,8},{11,9},{12,10},{13,11},... | collective-permute-start | bytes 1572872 | tf_op jit(solution)/shard_map/ppermute | solution.py:78
  31.1 3.6 %collective-permute-start.10 = (bf16[1024,256]{1,0:T(8,128)(2,1)S(1)}, bf16[1024,256]{1,0:T(8,128)(2,1)S(1)}, u32[]{:S(2)}, u32[]{:S(2)}) collective-permute-start(bf16[1024,256]{1,0:T(8,128)(2,1)S(1)} %constant_dynamic-slice_fusion.1), channel_id=1, source_target_pairs={{2,8},{3,9},{4,10},{5,11},{6,12},{7,13},{10,0},{11,1},{12,2},{13,3... | collective-permute-start | bytes 1572872 | tf_op jit(solution)/shard_map/ppermute | solution.py:78
  34.7 1.8 %broadcast_maximum_fusion.2 = bf16[1024,1024]{1,0:T(8,128)(2,1)S(1)} fusion(bf16[1024,1024]{1,0:T(8,128)(2,1)} %collective-permute-done.2), kind=kLoop, calls=%fused_computation.29 | loop fusion | flops 1048576 | bytes 4194304 | tf_op jit(solution)/shard_map/max | solution.py:132
  43.8 7.4 %collective-permute-done.7 = bf16[1024,256]{1,0:T(8,128)(2,1)S(1)} collective-permute-done((bf16[1024,256]{1,0:T(8,128)(2,1)S(1)}, bf16[1024,256]{1,0:T(8,128)(2,1)S(1)}, u32[]{:S(2)}, u32[]{:S(2)}) %collective-permute-start.7) | collective-permute-done | bytes 524320 | tf_op jit(solution)/shard_map/ppermute | solution.py:78
  52.6 10.3 %collective-permute-done.10 = bf16[1024,256]{1,0:T(8,128)(2,1)S(1)} collective-permute-done((bf16[1024,256]{1,0:T(8,128)(2,1)S(1)}, bf16[1024,256]{1,0:T(8,128)(2,1)S(1)}, u32[]{:S(2)}, u32[]{:S(2)}) %collective-permute-start.10) | collective-permute-done | bytes 524320 | tf_op jit(solution)/shard_map/ppermute | solution.py:78
  62.9 2.2 %collective-permute-start.5 = (bf16[1024,512]{1,0:T(8,128)(2,1)S(1)}, bf16[1024,512]{1,0:T(8,128)(2,1)S(1)}, u32[]{:S(2)}, u32[]{:S(2)}) collective-permute-start(bf16[1024,512]{1,0:T(8,128)(2,1)S(1)} %add_convert_fusion), channel_id=1, source_target_pairs={{16,0},{17,1},{18,2},{19,3},{20,4},{21,5},{22,6},{23,7},{24,8},{25... | collective-permute-start | bytes 3145736 | tf_op jit(solution)/shard_map/ppermute | solution.py:78
  70.3 1.5 %collective-permute-start.11 = (bf16[512,256]{1,0:T(8,128)(2,1)S(1)}, bf16[512,256]{1,0:T(8,128)(2,1)S(1)}, u32[]{:S(2)}, u32[]{:S(2)}) collective-permute-start(bf16[512,256]{1,0:T(8,128)(2,1)S(1)} %get-tuple-element.69), channel_id=1, source_target_pairs={{0,16},{1,17},{2,18},{3,19},{4,20},{5,21},{6,22},{7,23},{8,24},{9,... | collective-permute-start | bytes 786440 | tf_op jit(solution)/shard_map/ppermute | solution.py:78
  75.5 9.7 %collective-permute-done.12 = bf16[1024,256]{1,0:T(8,128)(2,1)S(1)} collective-permute-done((bf16[1024,256]{1,0:T(8,128)(2,1)S(1)}, bf16[1024,256]{1,0:T(8,128)(2,1)S(1)}, u32[]{:S(2)}, u32[]{:S(2)}) %collective-permute-start.12) | collective-permute-done | bytes 524320 | tf_op jit(solution)/shard_map/ppermute | solution.py:78
  89.6 1.9 %collective-permute-start.17 = (bf16[1024,256]{1,0:T(8,128)(2,1)S(1)}, bf16[1024,256]{1,0:T(8,128)(2,1)S(1)}, u32[]{:S(2)}, u32[]{:S(2)}) collective-permute-start(bf16[1024,256]{1,0:T(8,128)(2,1)S(1)} %fusion.5), channel_id=1, source_target_pairs={{18,16},{19,17},{20,18},{21,19},{22,20},{23,21},{26,24},{27,25},{2... | collective-permute-start | bytes 1572872 | tf_op jit(solution)/shard_map/ppermute | solution.py:78
  91.5 1.6 %collective-permute-start.16 = (bf16[1024,256]{1,0:T(8,128)(2,1)S(1)}, bf16[1024,256]{1,0:T(8,128)(2,1)S(1)}, u32[]{:S(2)}, u32[]{:S(2)}) collective-permute-start(bf16[1024,256]{1,0:T(8,128)(2,1)S(1)} %fusion.4), channel_id=1, source_target_pairs={{16,0},{17,1},{18,2},{19,3},{20,4},{21,5},{22,6},{23,7},{24,8},{25... | collective-permute-start | bytes 1572872 | tf_op jit(solution)/shard_map/ppermute | solution.py:78
  95.7 8.6 %collective-permute-done.18 = bf16[1024,256]{1,0:T(8,128)(2,1)S(1)} collective-permute-done((bf16[1024,256]{1,0:T(8,128)(2,1)S(1)}, bf16[1024,256]{1,0:T(8,128)(2,1)S(1)}, u32[]{:S(2)}, u32[]{:S(2)}) %collective-permute-start.18) | collective-permute-done | bytes 524320 | tf_op jit(solution)/shard_map/ppermute | solution.py:78
  106.9 1.9 %collective-permute-start.26 = (bf16[1024,256]{1,0:T(8,128)(2,1)S(1)}, bf16[1024,256]{1,0:T(8,128)(2,1)S(1)}, u32[]{:S(2)}, u32[]{:S(2)}) collective-permute-start(bf16[1024,256]{1,0:T(8,128)(2,1)S(1)} %fusion.3), channel_id=1, source_target_pairs={{18,16},{19,17},{20,18},{21,19},{22,20},{23,21},{26,24},{27,25},{2... | collective-permute-start | bytes 1572872 | tf_op jit(solution)/shard_map/ppermute | solution.py:78
  110.4 12.3 %collective-permute-done.20 = bf16[512,256]{1,0:T(8,128)(2,1)S(1)} collective-permute-done((bf16[512,256]{1,0:T(8,128)(2,1)S(1)}, bf16[512,256]{1,0:T(8,128)(2,1)S(1)}, u32[]{:S(2)}, u32[]{:S(2)}) %collective-permute-start.20) | collective-permute-done | bytes 262176 | tf_op jit(solution)/shard_map/ppermute | solution.py:78
  125.7 3.0 %collective-permute-start.21 = (bf16[1024,256]{1,0:T(8,128)(2,1)S(1)}, bf16[1024,256]{1,0:T(8,128)(2,1)S(1)}, u32[]{:S(2)}, u32[]{:S(2)}) collective-permute-start(bf16[1024,256]{1,0:T(8,128)(2,1)S(1)} %pad_maximum_fusion.1), channel_id=1, source_target_pairs={{0,8},{1,9},{2,10},{3,11},{4,12},{5,13},{6,14},{7,15},{8,0},{9,1},... | collective-permute-start | bytes 1572872 | tf_op jit(solution)/shard_map/ppermute | solution.py:78
  129.2 12.7 %collective-permute-start.28 = (bf16[1024,256]{1,0:T(8,128)(2,1)S(1)}, bf16[1024,256]{1,0:T(8,128)(2,1)S(1)}, u32[]{:S(2)}, u32[]{:S(2)}) collective-permute-start(bf16[1024,256]{1,0:T(8,128)(2,1)S(1)} %pad_maximum_fusion.3), channel_id=1, source_target_pairs={{0,8},{1,9},{2,10},{3,11},{4,12},{5,13},{6,14},{7,15},{8,0},{9,1},... | collective-permute-start | bytes 1572872 | tf_op jit(solution)/shard_map/ppermute | solution.py:78
  (99 shorter events, 38.8 us)
Async XLA Ops:
  11.9 19.2 %collective-permute-start.2 = (bf16[1024,1024]{1,0:T(8,128)(2,1)S(1)}, bf16[1024,1024]{1,0:T(8,128)(2,1)}, u32[]{:S(2)}, u32[]{:S(2)}) collective-permute-start(bf16[1024,1024]{1,0:T(8,128)(2,1)S(1)} %select_convert_fusion), channel_id=1, source_target_pairs={{0,8},{1,9},{2,10},{3,11},{4,12},{5,13},{6,14},{7,15},{8,0},{9,1},... | collective-permute-start | bytes 6291464 | tf_op jit(solution)/shard_map/ppermute | solution.py:78
  13.4 15.3 %collective-permute-start.3 = (bf16[1024,256]{1,0:T(8,128)(2,1)S(1)}, bf16[1024,256]{1,0:T(8,128)(2,1)S(1)}, u32[]{:S(2)}, u32[]{:S(2)}) collective-permute-start(bf16[1024,256]{1,0:T(8,128)(2,1)S(1)} %select_convert_fusion.1), channel_id=1, source_target_pairs={{2,0},{3,1},{4,2},{5,3},{6,4},{7,5},{10,8},{11,9},{12,10},{13,11},... | collective-permute-start | bytes 1572872 | tf_op jit(solution)/shard_map/ppermute | solution.py:78
  15.5 49.6 %collective-permute-start.14 = (bf16[1024,1024]{1,0:T(8,128)(2,1)S(1)}, bf16[1024,1024]{1,0:T(8,128)(2,1)S(1)}, u32[]{:S(2)}, u32[]{:S(2)}) collective-permute-start(bf16[1024,1024]{1,0:T(8,128)(2,1)S(1)} %select_convert_fusion), channel_id=1, source_target_pairs={{0,2},{1,3},{2,4},{3,5},{4,6},{5,7},{8,10},{9,11},{10,12},{11,13},... | collective-permute-start | bytes 6291464 | tf_op jit(solution)/shard_map/ppermute | solution.py:78
  18.9 22.1 %collective-permute-start.6 = (bf16[1024,256]{1,0:T(8,128)(2,1)S(1)}, bf16[1024,256]{1,0:T(8,128)(2,1)S(1)}, u32[]{:S(2)}, u32[]{:S(2)}) collective-permute-start(bf16[1024,256]{1,0:T(8,128)(2,1)S(1)} %constant_dynamic-slice_fusion.4), channel_id=1, source_target_pairs={{2,8},{3,9},{4,10},{5,11},{6,12},{7,13},{10,0},{11,1},{12,2},{13,3... | collective-permute-start | bytes 1572872 | tf_op jit(solution)/shard_map/ppermute | solution.py:78
  21.5 16.2 %collective-permute-start.4 = (bf16[1024,512]{1,0:T(8,128)(2,1)S(1)}, bf16[1024,512]{1,0:T(8,128)(2,1)S(1)}, u32[]{:S(2)}, u32[]{:S(2)}) collective-permute-start(bf16[1024,512]{1,0:T(8,128)(2,1)S(1)} %constant_dynamic-slice_fusion.3), channel_id=1, source_target_pairs={{0,8},{1,9},{2,10},{3,11},{4,12},{5,13},{6,14},{7,15},{8,0},{9,1},... | collective-permute-start | bytes 3145736 | tf_op jit(solution)/shard_map/ppermute | solution.py:78
  28.9 22.3 %collective-permute-start.7 = (bf16[1024,256]{1,0:T(8,128)(2,1)S(1)}, bf16[1024,256]{1,0:T(8,128)(2,1)S(1)}, u32[]{:S(2)}, u32[]{:S(2)}) collective-permute-start(bf16[1024,256]{1,0:T(8,128)(2,1)S(1)} %constant_dynamic-slice_fusion.2), channel_id=1, source_target_pairs={{2,0},{3,1},{4,2},{5,3},{6,4},{7,5},{10,8},{11,9},{12,10},{13,11},... | collective-permute-start | bytes 1572872 | tf_op jit(solution)/shard_map/ppermute | solution.py:78
  31.1 31.9 %collective-permute-start.10 = (bf16[1024,256]{1,0:T(8,128)(2,1)S(1)}, bf16[1024,256]{1,0:T(8,128)(2,1)S(1)}, u32[]{:S(2)}, u32[]{:S(2)}) collective-permute-start(bf16[1024,256]{1,0:T(8,128)(2,1)S(1)} %constant_dynamic-slice_fusion.1), channel_id=1, source_target_pairs={{2,8},{3,9},{4,10},{5,11},{6,12},{7,13},{10,0},{11,1},{12,2},{13,3... | collective-permute-start | bytes 1572872 | tf_op jit(solution)/shard_map/ppermute | solution.py:78
  37.8 29.2 %collective-permute-start.8 = (bf16[1024,256]{1,0:T(8,128)(2,1)S(1)}, bf16[1024,256]{1,0:T(8,128)(2,1)S(1)}, u32[]{:S(2)}, u32[]{:S(2)}) collective-permute-start(bf16[1024,256]{1,0:T(8,128)(2,1)S(1)} %broadcast_select_fusion.3), channel_id=1, source_target_pairs={{0,1},{1,0},{2,3},{3,2},{4,5},{5,4},{6,7},{7,6},{8,9},{9,8},{10,11... | collective-permute-start | bytes 1572872 | tf_op jit(solution)/shard_map/ppermute | solution.py:78
  41.0 25.2 %collective-permute-start.9 = (bf16[1024,256]{1,0:T(8,128)(2,1)S(1)}, bf16[1024,256]{1,0:T(8,128)(2,1)S(1)}, u32[]{:S(2)}, u32[]{:S(2)}) collective-permute-start(bf16[1024,256]{1,0:T(8,128)(2,1)S(1)} %broadcast_select_fusion.2), channel_id=1, source_target_pairs={{0,1},{1,8},{2,3},{3,10},{4,5},{5,12},{6,7},{7,14},{8,9},{9,0},{10... | collective-permute-start | bytes 1572872 | tf_op jit(solution)/shard_map/ppermute | solution.py:78
  51.3 24.1 %collective-permute-start.13 = (bf16[1024,256]{1,0:T(8,128)(2,1)S(1)}, bf16[1024,256]{1,0:T(8,128)(2,1)S(1)}, u32[]{:S(2)}, u32[]{:S(2)}) collective-permute-start(bf16[1024,256]{1,0:T(8,128)(2,1)S(1)} %broadcast_select_fusion.1), channel_id=1, source_target_pairs={{0,1},{1,0},{2,3},{3,2},{4,5},{5,4},{6,7},{7,6},{8,9},{9,8},{10,11... | collective-permute-start | bytes 1572872 | tf_op jit(solution)/shard_map/ppermute | solution.py:78
  62.9 30.3 %collective-permute-start.5 = (bf16[1024,512]{1,0:T(8,128)(2,1)S(1)}, bf16[1024,512]{1,0:T(8,128)(2,1)S(1)}, u32[]{:S(2)}, u32[]{:S(2)}) collective-permute-start(bf16[1024,512]{1,0:T(8,128)(2,1)S(1)} %add_convert_fusion), channel_id=1, source_target_pairs={{16,0},{17,1},{18,2},{19,3},{20,4},{21,5},{22,6},{23,7},{24,8},{25... | collective-permute-start | bytes 3145736 | tf_op jit(solution)/shard_map/ppermute | solution.py:78
  67.9 17.3 %collective-permute-start.12 = (bf16[1024,256]{1,0:T(8,128)(2,1)S(1)}, bf16[1024,256]{1,0:T(8,128)(2,1)S(1)}, u32[]{:S(2)}, u32[]{:S(2)}) collective-permute-start(bf16[1024,256]{1,0:T(8,128)(2,1)S(1)} %broadcast_select_fusion), channel_id=1, source_target_pairs={{0,1},{1,8},{2,3},{3,10},{4,5},{5,12},{6,7},{7,14},{8,9},{9,0},{10... | collective-permute-start | bytes 1572872 | tf_op jit(solution)/shard_map/ppermute | solution.py:78
  70.3 24.6 %collective-permute-start.11 = (bf16[512,256]{1,0:T(8,128)(2,1)S(1)}, bf16[512,256]{1,0:T(8,128)(2,1)S(1)}, u32[]{:S(2)}, u32[]{:S(2)}) collective-permute-start(bf16[512,256]{1,0:T(8,128)(2,1)S(1)} %get-tuple-element.69), channel_id=1, source_target_pairs={{0,16},{1,17},{2,18},{3,19},{4,20},{5,21},{6,22},{7,23},{8,24},{9,... | collective-permute-start | bytes 786440 | tf_op jit(solution)/shard_map/ppermute | solution.py:78
  88.3 16.0 %collective-permute-start.18 = (bf16[1024,256]{1,0:T(8,128)(2,1)S(1)}, bf16[1024,256]{1,0:T(8,128)(2,1)S(1)}, u32[]{:S(2)}, u32[]{:S(2)}) collective-permute-start(bf16[1024,256]{1,0:T(8,128)(2,1)S(1)} %fusion.5), channel_id=1, source_target_pairs={{2,16},{3,17},{4,18},{5,19},{6,20},{7,21},{10,24},{11,25},{12,26},... | collective-permute-start | bytes 1572872 | tf_op jit(solution)/shard_map/ppermute | solution.py:78
  89.6 16.0 %collective-permute-start.17 = (bf16[1024,256]{1,0:T(8,128)(2,1)S(1)}, bf16[1024,256]{1,0:T(8,128)(2,1)S(1)}, u32[]{:S(2)}, u32[]{:S(2)}) collective-permute-start(bf16[1024,256]{1,0:T(8,128)(2,1)S(1)} %fusion.5), channel_id=1, source_target_pairs={{18,16},{19,17},{20,18},{21,19},{22,20},{23,21},{26,24},{27,25},{2... | collective-permute-start | bytes 1572872 | tf_op jit(solution)/shard_map/ppermute | solution.py:78
  91.5 15.4 %collective-permute-start.16 = (bf16[1024,256]{1,0:T(8,128)(2,1)S(1)}, bf16[1024,256]{1,0:T(8,128)(2,1)S(1)}, u32[]{:S(2)}, u32[]{:S(2)}) collective-permute-start(bf16[1024,256]{1,0:T(8,128)(2,1)S(1)} %fusion.4), channel_id=1, source_target_pairs={{16,0},{17,1},{18,2},{19,3},{20,4},{21,5},{22,6},{23,7},{24,8},{25... | collective-permute-start | bytes 1572872 | tf_op jit(solution)/shard_map/ppermute | solution.py:78
  93.3 31.1 %collective-permute-start.25 = (bf16[1536,256]{1,0:T(8,128)(2,1)S(1)}, bf16[1536,256]{1,0:T(8,128)(2,1)S(1)}, u32[]{:S(2)}, u32[]{:S(2)}) collective-permute-start(bf16[1536,256]{1,0:T(8,128)(2,1)S(1)} %pad_maximum_fusion), channel_id=1, source_target_pairs={{16,0},{17,1},{18,2},{19,3},{20,4},{21,5},{22,6},{23,7},{24,8},{25... | collective-permute-start | bytes 2359304 | tf_op jit(solution)/shard_map/ppermute | solution.py:78
  104.3 18.4 %collective-permute-start.20 = (bf16[512,256]{1,0:T(8,128)(2,1)S(1)}, bf16[512,256]{1,0:T(8,128)(2,1)S(1)}, u32[]{:S(2)}, u32[]{:S(2)}) collective-permute-start(bf16[512,256]{1,0:T(8,128)(2,1)S(1)} %get-tuple-element.68), channel_id=1, source_target_pairs={{8,24},{9,25},{10,26},{11,27},{12,28},{13,29},{14,30},{15,31}} | collective-permute-start | bytes 786440 | tf_op jit(solution)/shard_map/ppermute | solution.py:78
  105.6 20.1 %collective-permute-start.27 = (bf16[1024,256]{1,0:T(8,128)(2,1)S(1)}, bf16[1024,256]{1,0:T(8,128)(2,1)S(1)}, u32[]{:S(2)}, u32[]{:S(2)}) collective-permute-start(bf16[1024,256]{1,0:T(8,128)(2,1)S(1)} %fusion.3), channel_id=1, source_target_pairs={{2,16},{3,17},{4,18},{5,19},{6,20},{7,21},{10,24},{11,25},{12,26},... | collective-permute-start | bytes 1572872 | tf_op jit(solution)/shard_map/ppermute | solution.py:78
  106.9 21.8 %collective-permute-start.26 = (bf16[1024,256]{1,0:T(8,128)(2,1)S(1)}, bf16[1024,256]{1,0:T(8,128)(2,1)S(1)}, u32[]{:S(2)}, u32[]{:S(2)}) collective-permute-start(bf16[1024,256]{1,0:T(8,128)(2,1)S(1)} %fusion.3), channel_id=1, source_target_pairs={{18,16},{19,17},{20,18},{21,19},{22,20},{23,21},{26,24},{27,25},{2... | collective-permute-start | bytes 1572872 | tf_op jit(solution)/shard_map/ppermute | solution.py:78
  109.1 19.8 %collective-permute-start.24 = (bf16[1024,256]{1,0:T(8,128)(2,1)S(1)}, bf16[1024,256]{1,0:T(8,128)(2,1)S(1)}, u32[]{:S(2)}, u32[]{:S(2)}) collective-permute-start(bf16[1024,256]{1,0:T(8,128)(2,1)S(1)} %copy-done.1), channel_id=1, source_target_pairs={{0,16},{1,17},{2,18},{3,19},{4,20},{5,21},{6,22},{7,23},{8,24},{9,... | collective-permute-start | bytes 1572872 | tf_op jit(solution)/shard_map/ppermute | solution.py:78
  122.7 20.8 %collective-permute-start.23 = (bf16[1024,256]{1,0:T(8,128)(2,1)S(1)}, bf16[1024,256]{1,0:T(8,128)(2,1)S(1)}, u32[]{:S(2)}, u32[]{:S(2)}) collective-permute-start(bf16[1024,256]{1,0:T(8,128)(2,1)S(1)} %pad_maximum_fusion.2), channel_id=1, source_target_pairs={{2,24},{3,25},{4,26},{5,27},{6,28},{7,29}} | collective-permute-start | bytes 1572872 | tf_op jit(solution)/shard_map/ppermute | solution.py:78
  124.4 19.2 %collective-permute-start.22 = (bf16[1024,256]{1,0:T(8,128)(2,1)S(1)}, bf16[1024,256]{1,0:T(8,128)(2,1)S(1)}, u32[]{:S(2)}, u32[]{:S(2)}) collective-permute-start(bf16[1024,256]{1,0:T(8,128)(2,1)S(1)} %pad_maximum_fusion.2), channel_id=1, source_target_pairs={{18,24},{19,25},{20,26},{21,27},{22,28},{23,29}} | collective-permute-start | bytes 1572872 | tf_op jit(solution)/shard_map/ppermute | solution.py:78
  125.7 17.9 %collective-permute-start.21 = (bf16[1024,256]{1,0:T(8,128)(2,1)S(1)}, bf16[1024,256]{1,0:T(8,128)(2,1)S(1)}, u32[]{:S(2)}, u32[]{:S(2)}) collective-permute-start(bf16[1024,256]{1,0:T(8,128)(2,1)S(1)} %pad_maximum_fusion.1), channel_id=1, source_target_pairs={{0,8},{1,9},{2,10},{3,11},{4,12},{5,13},{6,14},{7,15},{8,0},{9,1},... | collective-permute-start | bytes 1572872 | tf_op jit(solution)/shard_map/ppermute | solution.py:78
  (8 other events, 81.7 us)
